TPU v7x, 32 devices: a whole 2x2x4 slice. The times are simulated.
32 devices in a mesh: group: 8 (over y, x, core), shard: 4 (over z).
Axes of the slice: x: 2, y: 2, z: 4, core: 2. Of those that a mesh axis runs over, the one named last changes fastest.
Arguments:
- momentum: bfloat16 [8, 7168, 2048], P(None, ('group', 'shard'))
- gradient: bfloat16 [8, 7168, 2048], P(None, ('group', 'shard'))
- q_prev: bfloat16 [8, 3, 2048, 128], P('group', None, 'shard'), may hold values from -6 to 6
- owner_group: int32 [8], replicated, may hold values from 0 to 7, as said below
- group_counts: int32 [8], replicated, may hold values from 0 to 3, as said below
Outputs:
- momentum_next: bfloat16 [8, 7168, 2048], P(None, ('group', 'shard'))
- update: bfloat16 [8, 7168, 2048], P(None, ('group', 'shard'))
- q_next: bfloat16 [8, 3, 2048, 128], P('group', None, 'shard')
Inputs may be any that keep to these rules, and one draw needn't show every extreme that they name: `owner_group`: each group owns at most 3 experts and some group owns exactly 3; a group's experts fill its slots 0, 1, ... in increasing expert order. `group_counts`: entry g is the number of experts whose owner_group is g, except for one or two groups that own some experts, where it is one less; it equals 3 for some group that owns 3 experts.
All inputs are finite; a program needn't handle non-finite values.
Results may differ from a plain program's by a relative error of at most 0.0059.
Values may be sent and summed in bfloat16 or wider, within the bound.
A program may use at most 128 MiB of HBM per device.

v0:
```python
import math

import jax
import jax.numpy as jnp
from jax import lax
from jax.experimental import pallas as pl
from jax.experimental.pallas import tpu as pltpu
from jax.sharding import PartitionSpec as P

D = 7168
RANK = 128

stability_offset = 1e-06
momentum_decay = 0.6
AXES = ("group", "shard")


def owner_slots(owner_group):
    experts = owner_group.shape[0]
    expert_ids = jnp.arange(experts, dtype=jnp.int32)
    same_owner = owner_group[:, None] == owner_group[None, :]
    earlier = expert_ids[None, :] < expert_ids[:, None]
    return jnp.sum((same_owner & earlier).astype(jnp.int32), axis=1)


def exchange_sum(x, place, n, split, collective_id):
    rows, cols = x.shape[-2:]
    step = min(rows, 128)

    def kernel(x_ref, o_ref, landed, send_sem, recv_sem):
        me, peer = place()

        def copy(k):
            at = lax.rem(me + k, n)
            return pltpu.make_async_remote_copy(
                src_ref=x_ref.at[at] if split else x_ref,
                dst_ref=landed.at[k - 1],
                send_sem=send_sem.at[k - 1],
                recv_sem=recv_sem.at[k - 1],
                device_id=peer(at),
                device_id_type=pl.DeviceIdType.MESH,
            )

        barrier = pltpu.get_barrier_semaphore()

        @pl.loop(1, n)
        def _(k):
            pl.semaphore_signal(
                barrier,
                inc=1,
                device_id=peer(lax.rem(me + k, n)),
                device_id_type=pl.DeviceIdType.MESH,
            )

        pl.semaphore_wait(barrier, n - 1)

        @pl.loop(1, n)
        def _(k):
            copy(k).start()

        @pl.loop(1, n)
        def _(k):
            copy(k).wait()

        @pl.loop(0, rows // step)
        def _(i):
            span = pl.ds(pl.multiple_of(i * step, step), step)
            own = x_ref[me, span, :] if split else x_ref[span, :]
            total = own.astype(jnp.float32)
            for k in range(n - 1):
                total = total + landed[k, span, :].astype(jnp.float32)
            o_ref[span, :] = total.astype(o_ref.dtype)

    return pl.pallas_call(
        kernel,
        out_shape=jax.ShapeDtypeStruct((rows, cols), x.dtype),
        in_specs=[pl.BlockSpec(memory_space=pltpu.VMEM)],
        out_specs=pl.BlockSpec(memory_space=pltpu.VMEM),
        scratch_shapes=[
            pltpu.VMEM((n - 1, rows, cols), x.dtype),
            pltpu.SemaphoreType.DMA((n - 1,)),
            pltpu.SemaphoreType.DMA((n - 1,)),
        ],
        compiler_params=pltpu.CompilerParams(collective_id=collective_id, has_side_effects=True),
    )(x)


def on_group(stride, n):
    def place():
        g, s = lax.axis_index("group"), lax.axis_index("shard")
        digit = lax.rem(g // stride, n)
        return digit, lambda at: (g + (at - digit) * stride, s)

    return place


def on_shard():
    g, s = lax.axis_index("group"), lax.axis_index("shard")
    return s, lambda at: (g, at)


def on_all():
    width = lax.axis_size("shard")
    g, s = lax.axis_index("group"), lax.axis_index("shard")
    return g * width + s, lambda at: (at // width, lax.rem(at, width))


def scatter_over_group(x, first_id):
    groups = lax.axis_size("group")
    local, rows, cols = x.shape[0] // groups, x.shape[1], x.shape[2]
    pairs = x.reshape(groups // 2, 2, local * rows, cols).transpose(1, 0, 2, 3)
    pairs = pairs.reshape(2, groups // 2 * local * rows, cols)
    half = exchange_sum(pairs, on_group(1, 2), 2, True, first_id)
    half = half.reshape(groups // 2, local * rows, cols)
    out = exchange_sum(half, on_group(2, groups // 2), groups // 2, True, first_id + 1)
    return out.reshape(local, rows, cols)


def shards(momentum, gradient, q_prev, owner_group, group_counts):
    me = lax.axis_index("group")
    experts, block, hidden = momentum.shape
    cap, share_rows, rank = q_prev.shape[1:]
    slot_of = owner_slots(owner_group)
    keep = slot_of < group_counts[owner_group]
    mine = keep & (owner_group == me)

    pieces = jnp.zeros((experts, share_rows, rank), jnp.bfloat16)
    for j in range(cap):
        pick = mine & (slot_of == j)
        pieces = jnp.where(pick[:, None, None], q_prev[0, j][None], pieces)
    q_one = scatter_over_group(pieces, 0)
    q_shard = lax.all_gather(q_one, "shard", axis=1, tiled=True)
    q_full = lax.all_gather(q_shard, "group", axis=0, tiled=True)

    combined = (momentum.astype(jnp.float32) + gradient.astype(jnp.float32)).astype(jnp.bfloat16)
    left_raw = jnp.einsum("erh,ehk->erk", combined, q_full, preferred_element_type=jnp.float32)
    devices = lax.axis_size("group") * lax.axis_size("shard")
    squares = exchange_sum(jnp.sum(left_raw * left_raw, axis=1), on_all, devices, False, 2)
    left_unit = (left_raw * lax.rsqrt(squares + stability_offset)[:, None, :]).astype(jnp.bfloat16)
    part = jnp.einsum("erh,erk->ehk", combined, left_unit, preferred_element_type=jnp.float32)

    part = scatter_over_group(part.astype(jnp.bfloat16), 3)
    ring = lax.axis_size("shard")
    local = part.shape[0]
    part = part.reshape(local, ring, share_rows, rank).transpose(1, 0, 2, 3)
    part = part.reshape(ring, local * share_rows, rank)
    share = exchange_sum(part, on_shard, ring, True, 5).reshape(local, share_rows, rank)
    right = lax.all_gather(share, "shard", axis=1, tiled=True)
    right = lax.all_gather(right, "group", axis=0, tiled=True)

    right32 = right.astype(jnp.float32)
    scale = lax.rsqrt(jnp.mean(right32 * right32, axis=1) + stability_offset)
    q_new = (right32 * scale[:, None, :]).astype(jnp.bfloat16)
    update = (
        jnp.einsum("erk,ehk->erh", left_unit, q_new, preferred_element_type=jnp.float32)
        * math.sqrt(D / RANK)
    ).astype(jnp.bfloat16)
    low_rank = jnp.einsum("erk,ehk->erh", left_unit, right, preferred_element_type=jnp.float32)
    momentum_next = (
        combined.astype(jnp.float32) - (1.0 - momentum_decay) * low_rank
    ).astype(jnp.bfloat16)

    rows = lax.dynamic_slice_in_dim(q_new, lax.axis_index("shard") * share_rows, share_rows, axis=1)
    kept = []
    for j in range(cap):
        pick = mine & (slot_of == j)
        kept.append(jnp.sum(jnp.where(pick[:, None, None], rows, jnp.zeros_like(rows)), axis=0))
    return (momentum_next, update, jnp.stack(kept)[None])


def solution(mesh):
    return jax.shard_map(
        shards,
        mesh=mesh,
        in_specs=(
            P(None, AXES, None),
            P(None, AXES, None),
            P("group", None, "shard", None),
            P(),
            P(),
        ),
        out_specs=(P(None, AXES, None), P(None, AXES, None), P("group", None, "shard", None)),
        check_vma=False,
    )
```

profile of v0, /device:TPU:0, one launch (start us, length us, event | category | flops | bytes accessed | tf_op | source)
XLA Modules:
  0.0 257.1 jit_solution(8571426648664251801)
XLA Ops:
  7.2 0.0 copy-start
  7.2 0.0 all-gather.7.cloned.1.call-start
  7.2 0.9 convert_reduce_fusion
  8.1 0.7 compare_select_fusion
  8.8 0.0 copy-done
  8.8 0.6 gather_fusion
  9.5 0.7 compare_and_fusion.2
  10.1 0.1 broadcast_in_dim.133
  10.2 0.1 copy.18
  10.3 0.1 broadcast_bitcast_fusion
  10.4 0.1 broadcast_in_dim.124
  10.5 0.1 copy.17
  10.6 0.1 broadcast_bitcast_fusion.1
  10.7 0.1 broadcast_in_dim.115
  10.8 0.1 copy.16
  10.9 0.1 broadcast_bitcast_fusion.2
  11.0 1.1 slice_bitcast_fusion.2
  12.1 0.1 broadcast_in_dim.139
  12.2 0.1 broadcast_in_dim.130
  12.2 0.1 broadcast_in_dim.121
  12.3 4.0 %select_select_fusion.x_ref = bf16[2,2048,128]{2,1,0:T(8,128)(2,1)} fusion(pred[2,2048]{1,0:T(4,128)(4,1)S(1)} %bitcast.55, pred[2,2048]{1,0:T(4,128)(4,1)S(1)} %bitcast.56, pred[2,2048]{1,0:T(4,128)(4,1)S(1)} %bitcast.57, bf16[2048,128]{1,0:T(8,128)(2,1)S(1)} %bitcast.47, bf16[2048,128]{1,0:T(8,128)(2,1)S(1)} %bitcast.48, bf16[2048,128]{1,0:T(8,128)(2,1)S(1)} %bitcast.49), kind=kLoop, calls=%fused_computation.12 | loop fusion | flops 1572864 | bytes 2633728 | tf_op jit(solution)/shard_map/jit(_where)/select_n | solution.py:130
  16.3 4.3 %shard_map.76 = bf16[2048,128]{1,0:T(8,128)(2,1)} custom-call(bf16[2,2048,128]{2,1,0:T(8,128)(2,1)} %select_select_fusion.x_ref), custom_call_target="tpu_custom_call" | custom-call | tf_op jit(solution)/shard_map/pallas_call | solution.py:74
  20.6 12.6 %shard_map.77 = bf16[512,128]{1,0:T(8,128)(2,1)} custom-call(bf16[4,512,128]{2,1,0:T(8,128)(2,1)} %bitcast.50), custom_call_target="tpu_custom_call" | custom-call | tf_op jit(solution)/shard_map/pallas_call | solution.py:74
  33.2 17.8 %all-gather = bf16[2048,128]{1,0:T(8,128)(2,1)} all-gather(bf16[512,128]{1,0:T(8,128)(2,1)} %shard_map.77), channel_id=2, replica_groups=mesh['group'=8,'shard'=4] {'shard'}, dimensions={0}, use_global_device_ids=true | all-gather | bytes 655360 | tf_op jit(solution)/shard_map/all_gather | solution.py:132
  51.0 0.0 all-gather.7.cloned.1.call-update
  51.0 0.0 all-gather.9.cloned.1.call-start
  51.1 36.5 %all-gather.7.cloned.1.call-done = bf16[16384,128]{1,0:T(8,128)(2,1)} async-done(((bf16[2048,128]{1,0:T(8,128)(2,1)}), bf16[16384,128]{1,0:T(8,128)(2,1)}) %all-gather.7.cloned.1.call-update) | async-done | bytes 4194320 | tf_op jit(solution)/shard_map/all_gather | solution.py:133
  87.6 9.3 %multiply_reduce_fusion = (f32[8,128]{1,0:T(8,128)}, f32[8,224,128]{2,1,0:T(8,128)S(1)}) fusion(bf16[8,2048,128]{2,1,0:T(8,128)(2,1)} %bitcast.58, bf16[8,224,2048]{2,1,0:T(8,128)(2,1)} %param.6, bf16[8,224,2048]{2,1,0:T(8,128)(2,1)} %param.5), kind=kOutput, calls=%fused_computation.14 | convolution fusion | flops 954661888 | bytes 19795968 | tf_op jit(solution)/shard_map/erh,ehk->erk/dot_general | solution.py:136
  97.0 11.1 %shard_map.78 = f32[8,128]{1,0:T(8,128)} custom-call(f32[8,128]{1,0:T(8,128)} %get-tuple-element.13.x_ref), custom_call_target="tpu_custom_call" | custom-call | tf_op jit(solution)/shard_map/pallas_call | solution.py:74
  108.1 0.7 add_rsqrt_fusion.1
  108.8 0.1 multiply_convert_fusion.1
  108.9 10.6 %convolution_convert_fusion = bf16[8,2048,128]{2,1,0:T(8,128)(2,1)} fusion(bf16[8,224,128]{2,1,0:T(8,128)(2,1)S(1)} %multiply_convert_fusion.1, bf16[8,224,2048]{2,1,0:T(8,128)(2,1)} %param.6, bf16[8,224,2048]{2,1,0:T(8,128)(2,1)} %param.5), kind=kOutput, calls=%fused_computation.8 | convolution fusion | flops 956301312 | bytes 19333120 | tf_op jit(solution)/shard_map/erh,erk->ehk/dot_general | solution.py:140
  119.5 4.5 %copy.19 = bf16[4,2,2048,128]{3,2,0,1:T(8,128)(2,1)} copy(bf16[4,2,2048,128]{3,2,1,0:T(8,128)(2,1)} %bitcast.44) | data formatting | bytes 8388608 | tf_op jit(solution)/shard_map/reshape | solution.py:111
  124.0 8.5 %shard_map.79 = bf16[8192,128]{1,0:T(8,128)(2,1)} custom-call(bf16[2,8192,128]{2,1,0:T(8,128)(2,1)} %bitcast.45), custom_call_target="tpu_custom_call" | custom-call | tf_op jit(solution)/shard_map/pallas_call | solution.py:74
  132.5 28.9 %shard_map.80 = bf16[2048,128]{1,0:T(8,128)(2,1)} custom-call(bf16[4,2048,128]{2,1,0:T(8,128)(2,1)} %bitcast.46), custom_call_target="tpu_custom_call" | custom-call | tf_op jit(solution)/shard_map/pallas_call | solution.py:74
  161.4 14.8 %shard_map.81 = bf16[512,128]{1,0:T(8,128)(2,1)} custom-call(bf16[4,512,128]{2,1,0:T(8,128)(2,1)} %bitcast.51), custom_call_target="tpu_custom_call" | custom-call | tf_op jit(solution)/shard_map/pallas_call | solution.py:74
  176.2 18.4 %all-gather.2 = bf16[2048,128]{1,0:T(8,128)(2,1)} all-gather(bf16[512,128]{1,0:T(8,128)(2,1)} %shard_map.81), channel_id=4, replica_groups=mesh['group'=8,'shard'=4] {'shard'}, dimensions={0}, use_global_device_ids=true | all-gather | bytes 655360 | tf_op jit(solution)/shard_map/all_gather | solution.py:148
  194.6 0.0 all-gather.9.cloned.1.call-update
  194.6 36.1 %all-gather.9.cloned.1.call-done = bf16[16384,128]{1,0:T(8,128)(2,1)} async-done(((bf16[2048,128]{1,0:T(8,128)(2,1)}), bf16[16384,128]{1,0:T(8,128)(2,1)}) %all-gather.9.cloned.1.call-update) | async-done | bytes 4194320 | tf_op jit(solution)/shard_map/all_gather | solution.py:149
  230.8 0.0 copy-start.1
  230.8 11.3 %subtract_convert_fusion = bf16[8,224,2048]{2,1,0:T(8,128)(2,1)} fusion(bf16[8,224,128]{2,1,0:T(8,128)(2,1)S(1)} %multiply_convert_fusion.1, bf16[8,2048,128]{2,1,0:T(8,128)(2,1)} %bitcast.43, bf16[8,224,2048]{2,1,0:T(8,128)(2,1)} %param.6, bf16[8,224,2048]{2,1,0:T(8,128)(2,1)} %param.5), kind=kOutput, calls=%fused_computation.2 | convolution fusion | flops 968884224 | bytes 26673152 | tf_op jit(solution)/shard_map/erk,ehk->erh/dot_general | solution.py:158
  242.0 0.0 copy-done.1
  242.0 0.8 fusion
  242.9 0.8 fusion.1
  243.7 5.1 %multiply_convert_fusion = bf16[8,224,2048]{2,1,0:T(8,128)(2,1)} fusion(bf16[8,224,128]{2,1,0:T(8,128)(2,1)S(1)} %multiply_convert_fusion.1, bf16[8,2048,128]{2,1,0:T(8,128)(2,1)S(1)} %fusion.1), kind=kOutput, calls=%fused_computation.1 | convolution fusion | flops 946864128 | bytes 11993088 | tf_op jit(solution)/shard_map/erk,ehk->erh/dot_general | solution.py:155
  248.8 0.6 select_reduce_fusion.2
  249.4 0.8 maximum_bitcast_fusion
  (6 shorter events, 0.1 us)
Async XLA Ops:
  7.2 1.6 copy-start
  7.2 80.4 %all-gather.7.cloned.1.call-start = ((), (), s32[]{:S(2)}) async-start(), calls=%async_computation | async-start | bytes 4718592 | tf_op jit(solution)/shard_map/all_gather | solution.py:133
  51.0 179.7 %all-gather.9.cloned.1.call-start = ((), (), s32[]{:S(2)}) async-start(), calls=%async_computation.1 | async-start | bytes 4718592 | tf_op jit(solution)/shard_map/all_gather | solution.py:149
  230.8 11.3 %copy-start.1 = (bf16[16384,128]{1,0:T(8,128)(2,1)S(1)}, bf16[16384,128]{1,0:T(8,128)(2,1)}, u32[]{:S(2)}) copy-start(bf16[16384,128]{1,0:T(8,128)(2,1)} %all-gather.9.cloned.1.call-done) | copy-start | bytes 12582916
Sparse Core Ops, SparseCore 0:
  51.2 36.4 all-gather.6
  194.7 35.9 all-gather.8
where the time goes:
time: 258 us; the launch traced here: 257 us
  Pallas kernels  80.2 us (31%)
  waiting for transfers between devices  72.7 us (28%)
  matrix products  36.3 us (14%)
  blocking collectives  36.2 us (14%)
  between operations  14.2 us (6%)
  other arithmetic  10.1 us (4%)
  local copies, waits for them, and re-layouts  7.29 us (3%)
    pallas_call x6, Pallas kernels, exchange_sum(): pl.pallas_call(kernel, out_shape=jax.ShapeDtypeStruct((rows, cols), x.dty...  80.2 us
    all_gather x1, waiting for transfers between devices, shards(): q_full = lax.all_gather(q_shard, 'group', axis=0, tiled=True)  36.5 us
    all_gather x1, waiting for transfers between devices, shards(): right = lax.all_gather(right, 'group', axis=0, tiled=True)  36.1 us
    all_gather x1, blocking collectives, shards(): right = lax.all_gather(share, 'shard', axis=1, tiled=True)  18.4 us
    all_gather x1, blocking collectives, shards(): q_shard = lax.all_gather(q_one, 'shard', axis=1, tiled=True)  17.8 us
    dot_general x1, matrix products, shards(): jnp.einsum('erk,ehk->erh', left_unit, right, preferred_element_type=jnp.f...  11.3 us
    dot_general x1, matrix products, shards(): jnp.einsum('erh,erk->ehk', combined, left_unit, preferred_element_type=jn...  10.6 us
    dot_general x1, matrix products, shards(): jnp.einsum('erh,ehk->erk', combined, q_full, preferred_element_type=jnp.f...  9.35 us
  transfers between devices with their start and end apart: 2, of which 2 were waited for; matrix products, arithmetic and copies ran while one was open for 0% of the time, Pallas kernels for 0%

commit v1 on v0

v1 whole, which is shorter than its diff:
```python
import math

import jax
import jax.numpy as jnp
from jax import lax
from jax.experimental import pallas as pl
from jax.experimental.pallas import tpu as pltpu
from jax.sharding import PartitionSpec as P

D = 7168
RANK = 128

stability_offset = 1e-06
momentum_decay = 0.6
AXES = ("group", "shard")
LANES = 128
F32, BF16 = jnp.float32, jnp.bfloat16


def scalar_slot(owner_ref, e, experts, cap):
    own = owner_ref[e]
    slot = jnp.int32(0)
    for other in range(experts):
        hit = (owner_ref[other] == own) & (other < e)
        slot = slot + jnp.where(hit, 1, 0)
    return own, slot, jnp.minimum(slot, cap - 1)


def exchange(momentum, gradient, q_prev, owner_group, group_counts):
    experts, block, hidden = momentum.shape
    cap, share, rank = q_prev.shape[1:]
    groups, nz = lax.axis_size("group"), lax.axis_size("shard")
    m = groups // 2
    a = 2 ** ((m.bit_length() - 1) // 2)
    b = m // a
    rb = share // groups
    hb = hidden // LANES
    L = hb // m
    L2 = L // 2
    half = rank // 2
    subs = nz // L
    nr = half // subs
    q_view = q_prev.reshape(cap, 2, m, rb, rank)

    counts = [
        ("qcore", 1), ("qplane", m - 1), ("qz", nz - 1), ("qxy", a + b - 2),
        ("qdiag", 2 * (a - 1) * (b - 1)), ("qback", 1),
        ("s1", groups - 1), ("s2", nz - 1),
        ("rcore", 1), ("p1", a + b - 2), ("p2", a + b - 2), ("rz", nz - 1),
        ("gz", nz - 1), ("gxy", a + b - 2), ("gdiag", 2 * (a - 1) * (b - 1)), ("gback", 1),
    ]
    base, total = {}, 0
    for name, n in counts:
        base[name] = total
        total += n

    def kernel(
        mom, grad, q_in, owner_ref, counts_ref,
        comb_out, left_out, right_out,
        mom_buf, grad_buf, comb, q_own, qp, qc_land, qc, qp_land, Q,
        left_raw, left, s1, s1_land, s2, s2_land,
        pt, c_land, cs, p1a, p1b, s2a, s2b, p2a, p2b, ps, z_land, R,
        send, recv, load_sem, q_sem, comb_sem, left_sem, right_sem,
    ):
        g, s = lax.axis_index("group"), lax.axis_index("shard")
        c = lax.rem(g, 2)
        p = g // 2
        y, x = p // b, lax.rem(p, b)
        oc = 1 - c

        def up(v, k, n):
            return lax.rem(v + k, n)

        def down(v, k, n):
            return lax.rem(v + n - k, n)

        def copy(name, e, k, src, dst, device):
            return pltpu.make_async_remote_copy(
                src_ref=src, dst_ref=dst,
                send_sem=send.at[e, base[name] + k], recv_sem=recv.at[e, base[name] + k],
                device_id=device, device_id_type=pl.DeviceIdType.MESH,
            )

        def dev(yy, xx):
            return ((yy * b + xx) * 2 + c, s)

        core = (p * 2 + oc, s)

        def family(name, e):
            out = []
            if name == "qcore":
                out.append((qp.at[e, oc], qc_land.at[e], qc_land.at[e], core))
            elif name == "qplane":
                for k in range(1, m):
                    to = up(p, k, m)
                    out.append((qc.at[e, to], qp_land.at[e, k - 1], qp_land.at[e, k - 1], (to * 2 + c, s)))
            elif name == "qz":
                for k in range(1, nz):
                    here = Q.at[e, c, p, s]
                    out.append((here, here, Q.at[e, c, p, down(s, k, nz)], (g, up(s, k, nz))))
            elif name == "gz":
                def piece(at):
                    rows = pl.ds(pl.multiple_of((at // L) * nr, nr), nr)
                    return R.at[e, c, p * L + lax.rem(at, L), rows]
                for k in range(1, nz):
                    out.append((piece(s), piece(s), piece(down(s, k, nz)), (g, up(s, k, nz))))
            elif name in ("qxy", "gxy"):
                whole = q_place if name == "qxy" else r_place
                for k in range(1, a):
                    out.append((whole(e, y, x), whole(e, y, x), whole(e, down(y, k, a), x), dev(up(y, k, a), x)))
                for k in range(1, b):
                    out.append((whole(e, y, x), whole(e, y, x), whole(e, y, down(x, k, b)), dev(y, up(x, k, b))))
            elif name in ("qdiag", "gdiag"):
                part = q_half if name == "qdiag" else r_half
                for k in range(1, a):
                    for j in range(1, b):
                        xx = down(x, j, b)
                        out.append((part(e, y, xx, 0), part(e, y, xx, 0), part(e, down(y, k, a), xx, 0), dev(up(y, k, a), x)))
                for k in range(1, a):
                    for j in range(1, b):
                        yy = down(y, k, a)
                        out.append((part(e, yy, x, 1), part(e, yy, x, 1), part(e, yy, down(x, j, b), 1), dev(y, up(x, j, b))))
            elif name == "qback":
                out.append((Q.at[e, c], Q.at[e, c], Q.at[e, oc], core))
            elif name == "gback":
                out.append((R.at[e, c], R.at[e, c], R.at[e, oc], core))
            elif name == "s1":
                for k in range(1, groups):
                    out.append((s1.at[e], s1_land.at[e, k - 1], s1_land.at[e, k - 1], (up(g, k, groups), s)))
            elif name == "s2":
                for k in range(1, nz):
                    out.append((s2.at[e], s2_land.at[e, k - 1], s2_land.at[e, k - 1], (g, up(s, k, nz))))
            elif name == "rcore":
                out.append((pt.at[e, oc], c_land.at[e], c_land.at[e], core))
            elif name == "p1":
                for k in range(1, a):
                    out.append((cs.at[e, 0, up(y, k, a)], p1a.at[e, k - 1], p1a.at[e, k - 1], dev(up(y, k, a), x)))
                for k in range(1, b):
                    out.append((cs.at[e, 1, :, up(x, k, b)], p1b.at[e, k - 1], p1b.at[e, k - 1], dev(y, up(x, k, b))))
            elif name == "p2":
                for k in range(1, b):
                    out.append((s2a.at[e, up(x, k, b)], p2a.at[e, k - 1], p2a.at[e, k - 1], dev(y, up(x, k, b))))
                for k in range(1, a):
                    out.append((s2b.at[e, up(y, k, a)], p2b.at[e, k - 1], p2b.at[e, k - 1], dev(up(y, k, a), x)))
            elif name == "rz":
                for k in range(1, nz):
                    at = up(s, k, nz)
                    rows = pl.ds(pl.multiple_of((at // L) * nr, nr), nr)
                    out.append((ps.at[e, lax.rem(at, L), rows], z_land.at[e, k - 1], z_land.at[e, k - 1], (g, at)))
            return out

        def q_place(e, yy, xx):
            return Q.at[e, c, yy * b + xx]

        def q_half(e, yy, xx, h):
            return Q.at[e, c, yy * b + xx, pl.ds(h * (nz // 2), nz // 2)]

        def r_place(e, yy, xx):
            return R.at[e, c, pl.ds((yy * b + xx) * L, L)]

        def r_half(e, yy, xx, h):
            return R.at[e, c, pl.ds((yy * b + xx) * L + h * L2, L2)]

        def start(name, e):
            for k, (src, dst, _, device) in enumerate(family(name, e)):
                copy(name, e, k, src, dst, device).start()

        def arrived(name, e):
            for k, (src, _, dst, device) in enumerate(family(name, e)):
                copy(name, e, k, src, dst, device).wait_recv()

        def sent(name, e):
            for k, (src, dst, _, device) in enumerate(family(name, e)):
                copy(name, e, k, src, dst, device).wait_send()

        def loads(e):
            at = lax.rem(e, 2)
            return (
                pltpu.make_async_copy(mom.at[e], mom_buf.at[at], load_sem.at[at, 0]),
                pltpu.make_async_copy(grad.at[e], grad_buf.at[at], load_sem.at[at, 1]),
            )

        q_load = pltpu.make_async_copy(q_in, q_own, q_sem)
        q_load.start()
        for e in range(min(2, experts)):
            for one in loads(e):
                one.start()

        barrier = pltpu.get_barrier_semaphore()
        for k in range(1, groups):
            pl.semaphore_signal(barrier, inc=1, device_id=(up(g, k, groups), s), device_id_type=pl.DeviceIdType.MESH)
        for k in range(1, nz):
            pl.semaphore_signal(barrier, inc=1, device_id=(g, up(s, k, nz)), device_id_type=pl.DeviceIdType.MESH)

        q_load.wait()

        @pl.loop(0, experts)
        def _(e):
            own, slot, at = scalar_slot(owner_ref, e, experts, cap)
            live = (slot < counts_ref[own]) & (own == g)
            factor = jnp.where(live, 1.0, 0.0).astype(F32)
            for h in range(2):
                qp[e, h] = (q_own[at, h].astype(F32) * factor).astype(BF16)

        pl.semaphore_wait(barrier, groups + nz - 2)

        @pl.loop(0, experts)
        def _(e):
            start("qcore", e)

        def stage_q0(e):
            arrived("qcore", e)
            qc[e] = qp[e, c] + qc_land[e]
            start("qplane", e)

        def stage_q1(e):
            arrived("qplane", e)
            mine = qc[e, p]
            for k in range(m - 1):
                mine = mine + qp_land[e, k]
            Q[e, c, p, s] = mine
            start("qz", e)

        def stage_combine(e):
            for one in loads(e):
                one.wait()
            at = lax.rem(e, 2)
            comb[e] = (mom_buf[at].astype(F32) + grad_buf[at].astype(F32)).astype(BF16)
            pltpu.make_async_copy(comb.at[e], comb_out.at[e], comb_sem.at[e]).start()

            @pl.when(e + 2 < experts)
            def _():
                for one in loads(e + 2):
                    one.start()

        def relay(before, after):
            def stage(e):
                arrived(before, e)
                start(after, e)
            return stage

        def stage_left(e):
            arrived("qback", e)
            acc = jnp.zeros((block, rank), F32)
            span = share // 2
            for z in range(nz):
                for h in range(2):
                    rows = Q[e, h, :, z].reshape(span, rank)
                    lo = z * share + h * span
                    acc = acc + jnp.dot(comb[e, :, lo:lo + span], rows, preferred_element_type=F32)
            left_raw[e] = acc
            s1[e] = jnp.sum(acc * acc, axis=0, keepdims=True)
            start("s1", e)

        def stage_s(e):
            arrived("s1", e)
            tot = s1[e]
            for k in range(groups - 1):
                tot = tot + s1_land[e, k]
            s2[e] = tot
            start("s2", e)

        def stage_part(e):
            arrived("s2", e)
            tot = s2[e]
            for k in range(nz - 1):
                tot = tot + s2_land[e, k]
            unit = left_raw[e] * lax.rsqrt(tot + stability_offset)
            left[e] = unit.astype(BF16)
            pltpu.make_async_copy(left.at[e], left_out.at[e], left_sem.at[e]).start()
            unit_t = unit.T.astype(BF16)
            wide = 2 * LANES
            for j in range(hidden // wide):
                res = jnp.dot(unit_t, comb[e, :, j * wide:(j + 1) * wide], preferred_element_type=F32).astype(BF16)
                for i in range(2):
                    for h in range(2):
                        pt[e, h, 2 * j + i] = res[h * half:(h + 1) * half, i * LANES:(i + 1) * LANES]
            start("rcore", e)

        def stage_chip(e):
            arrived("rcore", e)
            for h in range(2):
                for i in range(L2):
                    for pp in range(m):
                        at = pp * L + h * L2 + i
                        cs[e, h, pp // b, pp % b, i] = (
                            pt[e, c, at].astype(F32) + c_land[e, at].astype(F32)
                        ).astype(BF16)
            start("p1", e)

        def stage_p1(e):
            arrived("p1", e)
            for i in range(b):
                tot = cs[e, 0, y, i].astype(F32)
                for k in range(a - 1):
                    tot = tot + p1a[e, k, i].astype(F32)
                s2a[e, i] = tot.astype(BF16)
            for i in range(a):
                tot = cs[e, 1, i, x].astype(F32)
                for k in range(b - 1):
                    tot = tot + p1b[e, k, i].astype(F32)
                s2b[e, i] = tot.astype(BF16)
            start("p2", e)

        def stage_p2(e):
            arrived("p2", e)
            tot = s2a[e, x].astype(F32)
            for k in range(b - 1):
                tot = tot + p2a[e, k].astype(F32)
            ps[e, 0:L2] = tot.astype(BF16)
            tot = s2b[e, y].astype(F32)
            for k in range(a - 1):
                tot = tot + p2b[e, k].astype(F32)
            ps[e, L2:L] = tot.astype(BF16)
            start("rz", e)

        def stage_rz(e):
            arrived("rz", e)
            rows = pl.ds(pl.multiple_of((s // L) * nr, nr), nr)
            tot = ps[e, lax.rem(s, L), rows].astype(F32)
            for k in range(nz - 1):
                tot = tot + z_land[e, k].astype(F32)
            R[e, c, p * L + lax.rem(s, L), rows] = tot.astype(BF16)
            start("gz", e)

        def stage_done(e):
            arrived("gback", e)
            pltpu.make_async_copy(R.at[e], right_out.at[e], right_sem.at[e]).start()
            for name, _ in counts:
                sent(name, e)

        stages = [
            (0, stage_q0), (1, stage_q1), (2, relay("qz", "qxy")), (3, relay("qxy", "qdiag")),
            (4, relay("qdiag", "qback")), (8, stage_chip), (9, stage_p1), (10, stage_p2),
            (11, stage_rz), (12, relay("gz", "gxy")), (13, relay("gxy", "gdiag")),
            (14, relay("gdiag", "gback")), (6, stage_s), (0, stage_combine), (7, stage_part),
            (5, stage_left), (15, stage_done),
        ]

        @pl.loop(0, experts + 15)
        def _(t):
            for offset, stage in stages:
                @pl.when((t >= offset) & (t < offset + experts))
                def _():
                    stage(t - offset)

        @pl.loop(0, experts)
        def _(e):
            pltpu.make_async_copy(comb.at[e], comb_out.at[e], comb_sem.at[e]).wait()
            pltpu.make_async_copy(left.at[e], left_out.at[e], left_sem.at[e]).wait()
            pltpu.make_async_copy(R.at[e], right_out.at[e], right_sem.at[e]).wait()

    E = experts
    hbm = pl.BlockSpec(memory_space=pl.ANY)
    smem = pl.BlockSpec(memory_space=pltpu.SMEM)
    return pl.pallas_call(
        kernel,
        name="exchange",
        out_shape=(
            jax.ShapeDtypeStruct((E, block, hidden), BF16),
            jax.ShapeDtypeStruct((E, block, rank), BF16),
            jax.ShapeDtypeStruct((E, 2, hb, half, LANES), BF16),
        ),
        in_specs=[hbm, hbm, hbm, smem, smem],
        out_specs=(hbm, hbm, hbm),
        scratch_shapes=[
            pltpu.VMEM((2, block, hidden), BF16),
            pltpu.VMEM((2, block, hidden), BF16),
            pltpu.VMEM((E, block, hidden), BF16),
            pltpu.VMEM((cap, 2, m, rb, rank), BF16),
            pltpu.VMEM((E, 2, m, rb, rank), BF16),
            pltpu.VMEM((E, m, rb, rank), BF16),
            pltpu.VMEM((E, m, rb, rank), BF16),
            pltpu.VMEM((E, m - 1, rb, rank), BF16),
            pltpu.VMEM((E, 2, m, nz, rb, rank), BF16),
            pltpu.VMEM((E, block, rank), F32),
            pltpu.VMEM((E, block, rank), BF16),
            pltpu.VMEM((E, 1, rank), F32),
            pltpu.VMEM((E, groups - 1, 1, rank), F32),
            pltpu.VMEM((E, 1, rank), F32),
            pltpu.VMEM((E, nz - 1, 1, rank), F32),
            pltpu.VMEM((E, 2, hb, half, LANES), BF16),
            pltpu.VMEM((E, hb, half, LANES), BF16),
            pltpu.VMEM((E, 2, a, b, L2, half, LANES), BF16),
            pltpu.VMEM((E, a - 1, b, L2, half, LANES), BF16),
            pltpu.VMEM((E, b - 1, a, L2, half, LANES), BF16),
            pltpu.VMEM((E, b, L2, half, LANES), BF16),
            pltpu.VMEM((E, a, L2, half, LANES), BF16),
            pltpu.VMEM((E, b - 1, L2, half, LANES), BF16),
            pltpu.VMEM((E, a - 1, L2, half, LANES), BF16),
            pltpu.VMEM((E, L, half, LANES), BF16),
            pltpu.VMEM((E, nz - 1, nr, LANES), BF16),
            pltpu.VMEM((E, 2, hb, half, LANES), BF16),
            pltpu.SemaphoreType.DMA((E, total)),
            pltpu.SemaphoreType.DMA((E, total)),
            pltpu.SemaphoreType.DMA((2, 2)),
            pltpu.SemaphoreType.DMA,
            pltpu.SemaphoreType.DMA((E,)),
            pltpu.SemaphoreType.DMA((E,)),
            pltpu.SemaphoreType.DMA((E,)),
        ],
        compiler_params=pltpu.CompilerParams(
            collective_id=0, has_side_effects=True, vmem_limit_bytes=63_000_000
        ),
    )(momentum, gradient, q_view, owner_group, group_counts)


def finish(combined, left, right, owner_group, group_counts, cap, share):
    experts, block, hidden = combined.shape
    rank = left.shape[2]
    hb, half = right.shape[2:4]
    own_blocks = share // LANES

    def kernel(owner_ref, counts_ref, comb, left_ref, right_ref, mom_out, upd_out, q_out, kept):
        e = pl.program_id(0)
        me, s = lax.axis_index("group"), lax.axis_index("shard")

        def block_of(i):
            return jnp.concatenate([right_ref[0, 0, i], right_ref[0, 1, i]], axis=0).astype(F32)

        squares = jnp.zeros((rank, LANES), F32)
        for i in range(hb):
            one = block_of(i)
            squares = squares + one * one
        scale = lax.rsqrt(jnp.sum(squares, axis=1, keepdims=True) / hidden + stability_offset)

        unit = left_ref[0]
        for j in range(hb // 2):
            raw = jnp.concatenate([block_of(2 * j), block_of(2 * j + 1)], axis=1)
            span = slice(2 * j * LANES, (2 * j + 2) * LANES)
            low = jnp.dot(unit, raw.astype(BF16), preferred_element_type=F32)
            mom_out[0, :, span] = (
                comb[0, :, span].astype(F32) - (1.0 - momentum_decay) * low
            ).astype(BF16)
            new = (raw * scale).astype(BF16)
            upd_out[0, :, span] = (
                jnp.dot(unit, new, preferred_element_type=F32) * math.sqrt(D / RANK)
            ).astype(BF16)

        @pl.when(e == 0)
        def _():
            kept[...] = jnp.zeros_like(kept)

        own, slot, at = scalar_slot(owner_ref, e, experts, cap)

        @pl.when((slot < counts_ref[own]) & (own == me))
        def _():
            for i in range(own_blocks):
                kept[at, i] = (block_of(s * own_blocks + i) * scale).astype(BF16).astype(F32)

        @pl.when(e == experts - 1)
        def _():
            for j in range(cap):
                for i in range(own_blocks):
                    q_out[0, j, i * LANES:(i + 1) * LANES, :] = kept[j, i].T.astype(BF16)

    smem = pl.BlockSpec(memory_space=pltpu.SMEM)
    row = pl.BlockSpec((1, block, hidden), lambda e: (e, 0, 0))
    return pl.pallas_call(
        kernel,
        name="finish",
        grid=(experts,),
        out_shape=(
            jax.ShapeDtypeStruct(combined.shape, BF16),
            jax.ShapeDtypeStruct(combined.shape, BF16),
            jax.ShapeDtypeStruct((1, cap, share, rank), BF16),
        ),
        in_specs=[
            smem, smem, row,
            pl.BlockSpec((1, block, rank), lambda e: (e, 0, 0)),
            pl.BlockSpec((1, 2, hb, half, LANES), lambda e: (e, 0, 0, 0, 0)),
        ],
        out_specs=(row, row, pl.BlockSpec((1, cap, share, rank), lambda e: (0, 0, 0, 0))),
        scratch_shapes=[pltpu.VMEM((cap, own_blocks, rank, LANES), F32)],
        compiler_params=pltpu.CompilerParams(dimension_semantics=("arbitrary",)),
    )(owner_group, group_counts, combined, left, right)


def shards(momentum, gradient, q_prev, owner_group, group_counts):
    cap, share = q_prev.shape[1:3]
    combined, left, right = exchange(momentum, gradient, q_prev, owner_group, group_counts)
    return finish(combined, left, right, owner_group, group_counts, cap, share)


def solution(mesh):
    return jax.shard_map(
        shards,
        mesh=mesh,
        in_specs=(
            P(None, AXES, None),
            P(None, AXES, None),
            P("group", None, "shard", None),
            P(),
            P(),
        ),
        out_specs=(P(None, AXES, None), P(None, AXES, None), P("group", None, "shard", None)),
        check_vma=False,
    )
```

time: 258 us -> 106 us (0.41)
  waiting for transfers between devices: 72.7 us -> 0 us
  matrix products: 36.3 us -> 0 us
  blocking collectives: 36.2 us -> 0 us
  Pallas kernels: 80.2 us -> 105 us
  between operations: 14.2 us -> 0.64 us
  other arithmetic: 10.1 us -> 0 us
  local copies, waits for them, and re-layouts: 7.29 us -> 0 us
    all_gather x2 -> x0, waiting for transfers between devices: 72.7 us -> none  [the longest x1 36.5 us: shards(): q_full = lax.all_gather(q_shard, 'group', axis=0, tiled=True)]
    dot_general x4 -> x0, matrix products: 36.3 us -> none  [the longest x1 11.3 us: shards(): jnp.einsum('erk,ehk->erh', left_unit, right, preferred_element_type=jnp.f...]
    all_gather x2 -> x0, blocking collectives: 36.2 us -> none  [the longest x1 18.4 us: shards(): right = lax.all_gather(share, 'shard', axis=1, tiled=True)]
    pallas_call x6 -> x2, Pallas kernels: 80.2 us -> 105 us  [the longest x1 90.3 us: exchange(): pl.pallas_call(kernel, name='exchange', out_shape=(jax.ShapeDtypeStruct((...]
    select_n x2 -> x0, other arithmetic: 4.67 us -> none  [the longest x1 4.01 us: shards(): pieces = jnp.where(pick[:, None, None], q_prev[0, j][None], pieces)]
    reshape x1 -> x0, local copies, waits for them, and re-layouts: 4.5 us -> none  [scatter_over_group(): pairs = x.reshape(groups // 2, 2, local * rows, cols).transpose(1, 0, 2, 3)]
  transfers between devices with their start and end apart: 2 -> 0, of which waited for: 2 -> 0; matrix products, arithmetic and copies ran while one was open for 0% -> 0% of each run, Pallas kernels for 0% -> 0%
where the time goes in v1:
time: 106 us; the launch traced here: 105 us
  Pallas kernels  105 us (99%)
    pallas_call x1, Pallas kernels, exchange(): pl.pallas_call(kernel, name='exchange', out_shape=(jax.ShapeDtypeStruct((...  90.3 us
    pallas_call x1, Pallas kernels, finish(): pl.pallas_call(kernel, name='finish', grid=(experts,), out_shape=(jax.Sha...  14.6 us

profile of v1, /device:TPU:0, one launch (start us, length us, event | category | flops | bytes accessed | tf_op | source)
XLA Modules:
  0.0 105.5 jit_solution(8419407276156411614)
XLA Ops:
  0.6 90.3 %exchange.1 = (bf16[8,224,2048]{2,1,0:T(8,128)(2,1)}, bf16[8,224,128]{2,1,0:T(8,128)(2,1)}, bf16[8,2,16,64,128]{4,3,2,1,0:T(8,128)(2,1)}) custom-call(bf16[8,224,2048]{2,1,0:T(8,128)(2,1)} %mom.1, bf16[8,224,2048]{2,1,0:T(8,128)(2,1)} %grad.1, bf16[3,2,4,64,128]{4,3,2,1,0:T(8,128)(2,1)} %bitcast.1, s32[8]{0:T(128)} %owner_ref.3, s32[8]{0:T(128)} %counts_ref.3), custom_call_target="tpu_custom_call" | custom-call | tf_op jit(solution)/shard_map/exchange/pallas_call | solution.py:356
  90.9 14.6 %finish.1 = (bf16[8,224,2048]{2,1,0:T(8,128)(2,1)}, bf16[8,224,2048]{2,1,0:T(8,128)(2,1)}, bf16[1,3,512,128]{3,2,1,0:T(8,128)(2,1)}) custom-call(s32[8]{0:T(128)} %owner_ref.3, s32[8]{0:T(128)} %counts_ref.3, bf16[8,224,2048]{2,1,0:T(8,128)(2,1)} %get-tuple-element.6.comb, bf16[8,224,128]{2,1,0:T(8,128)(2,1)} %get-tuple-element.7.left_ref, ...), custom_call_target="tpu_custom_call" | custom-call | tf_op jit(solution)/shard_map/finish/pallas_call | solution.py:459

commit v2 on v1

--- a/solution.py
+++ b/solution.py
@@ -14,7 +14,14 @@
 momentum_decay = 0.6
 AXES = ("group", "shard")
 LANES = 128
+VMEM_BYTES = 67_043_328
 F32, BF16 = jnp.float32, jnp.bfloat16
+
+
+def vmem_bytes(ref):
+    rows = -(-ref.shape[-2] // 8) * 8 if ref.shape[-2] > 1 else 1
+    lanes = -(-ref.shape[-1] // LANES) * LANES
+    return math.prod(ref.shape[:-2]) * rows * lanes * jnp.dtype(ref.dtype).itemsize
 
 
 def scalar_slot(owner_ref, e, experts, cap):
@@ -45,7 +52,7 @@
     counts = [
         ("qcore", 1), ("qplane", m - 1), ("qz", nz - 1), ("qxy", a + b - 2),
         ("qdiag", 2 * (a - 1) * (b - 1)), ("qback", 1),
-        ("s1", groups - 1), ("s2", nz - 1),
+        ("ncore", 1), ("n1", a + b - 2), ("n2", a + b - 2), ("nz", nz - 1),
         ("rcore", 1), ("p1", a + b - 2), ("p2", a + b - 2), ("rz", nz - 1),
         ("gz", nz - 1), ("gxy", a + b - 2), ("gdiag", 2 * (a - 1) * (b - 1)), ("gback", 1),
     ]
@@ -55,12 +62,12 @@
         total += n
 
     def kernel(
-        mom, grad, q_in, owner_ref, counts_ref,
-        comb_out, left_out, right_out,
-        mom_buf, grad_buf, comb, q_own, qp, qc_land, qc, qp_land, Q,
-        left_raw, left, s1, s1_land, s2, s2_land,
+        mom, grad, q_in, owner_in, counts_in,
+        comb, left, right_out,
+        mom_buf, grad_buf, q_own, qp, qc_land, qc, qp_land, Q,
+        left_raw, n_own, nc_land, n_chip, n1_land, n_a, n_b, n2_land, n_place, nz_land, weights,
         pt, c_land, cs, p1a, p1b, s2a, s2b, p2a, p2b, ps, z_land, R,
-        send, recv, load_sem, q_sem, comb_sem, left_sem, right_sem,
+        send, recv, load_sem, owner_ref, counts_ref, small_sem,
     ):
         g, s = lax.axis_index("group"), lax.axis_index("shard")
         c = lax.rem(g, 2)
@@ -124,12 +131,23 @@
                 out.append((Q.at[e, c], Q.at[e, c], Q.at[e, oc], core))
             elif name == "gback":
                 out.append((R.at[e, c], R.at[e, c], R.at[e, oc], core))
-            elif name == "s1":
-                for k in range(1, groups):
-                    out.append((s1.at[e], s1_land.at[e, k - 1], s1_land.at[e, k - 1], (up(g, k, groups), s)))
-            elif name == "s2":
+            elif name == "ncore":
+                out.append((n_own.at[e], nc_land.at[e], nc_land.at[e], core))
+            elif name == "n1":
+                for k in range(1, a):
+                    out.append((n_chip.at[e], n1_land.at[e, k - 1], n1_land.at[e, k - 1], dev(up(y, k, a), x)))
+                for k in range(1, b):
+                    at = n1_land.at[e, a - 1 + k - 1]
+                    out.append((n_chip.at[e], at, at, dev(y, up(x, k, b))))
+            elif name == "n2":
+                for k in range(1, b):
+                    out.append((n_a.at[e], n2_land.at[e, k - 1], n2_land.at[e, k - 1], dev(y, up(x, k, b))))
+                for k in range(1, a):
+                    at = n2_land.at[e, b - 1 + k - 1]
+                    out.append((n_b.at[e], at, at, dev(up(y, k, a), x)))
+            elif name == "nz":
                 for k in range(1, nz):
-                    out.append((s2.at[e], s2_land.at[e, k - 1], s2_land.at[e, k - 1], (g, up(s, k, nz))))
+                    out.append((n_place.at[e], nz_land.at[e, k - 1], nz_land.at[e, k - 1], (g, up(s, k, nz))))
             elif name == "rcore":
                 out.append((pt.at[e, oc], c_land.at[e], c_land.at[e], core))
             elif name == "p1":
@@ -180,8 +198,13 @@
                 pltpu.make_async_copy(grad.at[e], grad_buf.at[at], load_sem.at[at, 1]),
             )
 
-        q_load = pltpu.make_async_copy(q_in, q_own, q_sem)
-        q_load.start()
+        small = [
+            pltpu.make_async_copy(q_in, q_own, small_sem.at[0]),
+            pltpu.make_async_copy(owner_in, owner_ref, small_sem.at[1]),
+            pltpu.make_async_copy(counts_in, counts_ref, small_sem.at[2]),
+        ]
+        for one in small:
+            one.start()
         for e in range(min(2, experts)):
             for one in loads(e):
                 one.start()
@@ -192,7 +215,8 @@
         for k in range(1, nz):
             pl.semaphore_signal(barrier, inc=1, device_id=(g, up(s, k, nz)), device_id_type=pl.DeviceIdType.MESH)
 
-        q_load.wait()
+        for one in small:
+            one.wait()
 
         @pl.loop(0, experts)
         def _(e):
@@ -226,7 +250,6 @@
                 one.wait()
             at = lax.rem(e, 2)
             comb[e] = (mom_buf[at].astype(F32) + grad_buf[at].astype(F32)).astype(BF16)
-            pltpu.make_async_copy(comb.at[e], comb_out.at[e], comb_sem.at[e]).start()
 
             @pl.when(e + 2 < experts)
             def _():
@@ -238,6 +261,18 @@
                 arrived(before, e)
                 start(after, e)
             return stage
+
+        def merge(parts):
+            tot = parts[0]
+            for one in parts[1:]:
+                tot = tot + one
+            scale = lax.rsqrt(tot + stability_offset)
+            finite = tot < jnp.inf
+            rows = [jnp.where(finite, jnp.sqrt(one + stability_offset) * scale, 0.0) for one in parts]
+            rows += [jnp.zeros_like(tot)] * (8 - len(rows))
+            weights[...] = jnp.concatenate(rows, axis=0).T
+            mine = weights[pl.ds(pl.multiple_of(c * half, half), half), :]
+            return tot, [mine[:, k:k + 1] for k in range(len(parts))]
 
         def stage_left(e):
             arrived("qback", e)
@@ -249,26 +284,10 @@
                     lo = z * share + h * span
                     acc = acc + jnp.dot(comb[e, :, lo:lo + span], rows, preferred_element_type=F32)
             left_raw[e] = acc
-            s1[e] = jnp.sum(acc * acc, axis=0, keepdims=True)
-            start("s1", e)
-
-        def stage_s(e):
-            arrived("s1", e)
-            tot = s1[e]
-            for k in range(groups - 1):
-                tot = tot + s1_land[e, k]
-            s2[e] = tot
-            start("s2", e)
-
-        def stage_part(e):
-            arrived("s2", e)
-            tot = s2[e]
-            for k in range(nz - 1):
-                tot = tot + s2_land[e, k]
-            unit = left_raw[e] * lax.rsqrt(tot + stability_offset)
-            left[e] = unit.astype(BF16)
-            pltpu.make_async_copy(left.at[e], left_out.at[e], left_sem.at[e]).start()
-            unit_t = unit.T.astype(BF16)
+            squares = jnp.sum(acc * acc, axis=0, keepdims=True)
+            n_own[e] = squares
+            start("ncore", e)
+            unit_t = (acc * lax.rsqrt(squares + stability_offset)).T.astype(BF16)
             wide = 2 * LANES
             for j in range(hidden // wide):
                 res = jnp.dot(unit_t, comb[e, :, j * wide:(j + 1) * wide], preferred_element_type=F32).astype(BF16)
@@ -278,81 +297,141 @@
             start("rcore", e)
 
         def stage_chip(e):
+            arrived("ncore", e)
+            tot, (w_own, w_land) = merge([n_own[e], nc_land[e]])
+            n_chip[e] = tot
+            start("n1", e)
             arrived("rcore", e)
             for h in range(2):
                 for i in range(L2):
                     for pp in range(m):
                         at = pp * L + h * L2 + i
                         cs[e, h, pp // b, pp % b, i] = (
-                            pt[e, c, at].astype(F32) + c_land[e, at].astype(F32)
+                            pt[e, c, at].astype(F32) * w_own + c_land[e, at].astype(F32) * w_land
                         ).astype(BF16)
             start("p1", e)
 
         def stage_p1(e):
+            arrived("n1", e)
+            tot_a, w_a = merge([n_chip[e]] + [n1_land[e, k] for k in range(a - 1)])
+            tot_b, w_b = merge([n_chip[e]] + [n1_land[e, a - 1 + k] for k in range(b - 1)])
+            n_a[e] = tot_a
+            n_b[e] = tot_b
+            start("n2", e)
             arrived("p1", e)
             for i in range(b):
-                tot = cs[e, 0, y, i].astype(F32)
+                tot = cs[e, 0, y, i].astype(F32) * w_a[0]
                 for k in range(a - 1):
-                    tot = tot + p1a[e, k, i].astype(F32)
+                    tot = tot + p1a[e, k, i].astype(F32) * w_a[k + 1]
                 s2a[e, i] = tot.astype(BF16)
             for i in range(a):
-                tot = cs[e, 1, i, x].astype(F32)
+                tot = cs[e, 1, i, x].astype(F32) * w_b[0]
                 for k in range(b - 1):
-                    tot = tot + p1b[e, k, i].astype(F32)
+                    tot = tot + p1b[e, k, i].astype(F32) * w_b[k + 1]
                 s2b[e, i] = tot.astype(BF16)
             start("p2", e)
 
         def stage_p2(e):
+            arrived("n2", e)
+            tot_a, w_a = merge([n_a[e]] + [n2_land[e, k] for k in range(b - 1)])
+            _, w_b = merge([n_b[e]] + [n2_land[e, b - 1 + k] for k in range(a - 1)])
+            n_place[e] = tot_a
+            start("nz", e)
             arrived("p2", e)
-            tot = s2a[e, x].astype(F32)
+            tot = s2a[e, x].astype(F32) * w_a[0]
             for k in range(b - 1):
-                tot = tot + p2a[e, k].astype(F32)
+                tot = tot + p2a[e, k].astype(F32) * w_a[k + 1]
             ps[e, 0:L2] = tot.astype(BF16)
-            tot = s2b[e, y].astype(F32)
+            tot = s2b[e, y].astype(F32) * w_b[0]
             for k in range(a - 1):
-                tot = tot + p2b[e, k].astype(F32)
+                tot = tot + p2b[e, k].astype(F32) * w_b[k + 1]
             ps[e, L2:L] = tot.astype(BF16)
             start("rz", e)
 
         def stage_rz(e):
+            arrived("nz", e)
+            at = pl.multiple_of((s // L) * nr, nr)
+            total_squares, w = merge([n_place[e]] + [nz_land[e, k] for k in range(nz - 1)])
+            sub = pl.ds(pl.multiple_of(c * half + at, nr), nr)
+            w = [weights[sub, k:k + 1] for k in range(nz)]
             arrived("rz", e)
-            rows = pl.ds(pl.multiple_of((s // L) * nr, nr), nr)
-            tot = ps[e, lax.rem(s, L), rows].astype(F32)
+            rows = pl.ds(at, nr)
+            tot = ps[e, lax.rem(s, L), rows].astype(F32) * w[0]
             for k in range(nz - 1):
-                tot = tot + z_land[e, k].astype(F32)
+                tot = tot + z_land[e, k].astype(F32) * w[k + 1]
             R[e, c, p * L + lax.rem(s, L), rows] = tot.astype(BF16)
             start("gz", e)
+            left[e] = (left_raw[e] * lax.rsqrt(total_squares + stability_offset)).astype(BF16)
 
         def stage_done(e):
             arrived("gback", e)
-            pltpu.make_async_copy(R.at[e], right_out.at[e], right_sem.at[e]).start()
+            for h in range(2):
+                right_out[e, h] = R[e, h]
             for name, _ in counts:
                 sent(name, e)
 
         stages = [
-            (0, stage_q0), (1, stage_q1), (2, relay("qz", "qxy")), (3, relay("qxy", "qdiag")),
-            (4, relay("qdiag", "qback")), (8, stage_chip), (9, stage_p1), (10, stage_p2),
-            (11, stage_rz), (12, relay("gz", "gxy")), (13, relay("gxy", "gdiag")),
-            (14, relay("gdiag", "gback")), (6, stage_s), (0, stage_combine), (7, stage_part),
-            (5, stage_left), (15, stage_done),
+            (0, stage_q0),
+            (2, stage_q1),
+            (4, relay("qz", "qxy")),
+            (6, relay("qxy", "qdiag")),
+            (8, relay("qdiag", "qback")),
+            (0, stage_combine),
+            (9, stage_left),
+            (10, stage_chip),
+            (11, stage_p1),
+            (12, stage_p2),
+            (14, stage_rz),
+            (16, relay("gz", "gxy")),
+            (17, relay("gxy", "gdiag")),
+            (18, relay("gdiag", "gback")),
+            (19, stage_done),
         ]
 
-        @pl.loop(0, experts + 15)
+        @pl.loop(0, experts + 19)
         def _(t):
             for offset, stage in stages:
                 @pl.when((t >= offset) & (t < offset + experts))
                 def _():
                     stage(t - offset)
 
-        @pl.loop(0, experts)
-        def _(e):
-            pltpu.make_async_copy(comb.at[e], comb_out.at[e], comb_sem.at[e]).wait()
-            pltpu.make_async_copy(left.at[e], left_out.at[e], left_sem.at[e]).wait()
-            pltpu.make_async_copy(R.at[e], right_out.at[e], right_sem.at[e]).wait()
-
     E = experts
-    hbm = pl.BlockSpec(memory_space=pl.ANY)
-    smem = pl.BlockSpec(memory_space=pltpu.SMEM)
+    scratch = [
+        pltpu.VMEM((2, block, hidden), BF16),
+        pltpu.VMEM((2, block, hidden), BF16),
+        pltpu.VMEM((cap, 2, m, rb, rank), BF16),
+        pltpu.VMEM((E, 2, m, rb, rank), BF16),
+        pltpu.VMEM((E, m, rb, rank), BF16),
+        pltpu.VMEM((E, m, rb, rank), BF16),
+        pltpu.VMEM((E, m - 1, rb, rank), BF16),
+        pltpu.VMEM((E, 2, m, nz, rb, rank), BF16),
+        pltpu.VMEM((E, block, rank), F32),
+        pltpu.VMEM((E, 1, rank), F32),
+        pltpu.VMEM((E, 1, rank), F32),
+        pltpu.VMEM((E, 1, rank), F32),
+        pltpu.VMEM((E, a + b - 2, 1, rank), F32),
+        pltpu.VMEM((E, 1, rank), F32),
+        pltpu.VMEM((E, 1, rank), F32),
+        pltpu.VMEM((E, a + b - 2, 1, rank), F32),
+        pltpu.VMEM((E, 1, rank), F32),
+        pltpu.VMEM((E, nz - 1, 1, rank), F32),
+        pltpu.VMEM((rank, 8), F32),
+        pltpu.VMEM((E, 2, hb, half, LANES), BF16),
+        pltpu.VMEM((E, hb, half, LANES), BF16),
+        pltpu.VMEM((E, 2, a, b, L2, half, LANES), BF16),
+        pltpu.VMEM((E, a - 1, b, L2, half, LANES), BF16),
+        pltpu.VMEM((E, b - 1, a, L2, half, LANES), BF16),
+        pltpu.VMEM((E, b, L2, half, LANES), BF16),
+        pltpu.VMEM((E, a, L2, half, LANES), BF16),
+        pltpu.VMEM((E, b - 1, L2, half, LANES), BF16),
+        pltpu.VMEM((E, a - 1, L2, half, LANES), BF16),
+        pltpu.VMEM((E, L, half, LANES), BF16),
+        pltpu.VMEM((E, nz - 1, nr, LANES), BF16),
+        pltpu.VMEM((E, 2, hb, half, LANES), BF16),
+    ]
+    outputs = 2 * E * (block * (hidden + rank) + hidden * rank)
+    limit = min(VMEM_BYTES, sum(map(vmem_bytes, scratch)) + outputs + 1_500_000)
+    hbm = pl.BlockSpec(memory_space=pltpu.HBM)
     return pl.pallas_call(
         kernel,
         name="exchange",
@@ -361,46 +440,18 @@
             jax.ShapeDtypeStruct((E, block, rank), BF16),
             jax.ShapeDtypeStruct((E, 2, hb, half, LANES), BF16),
         ),
-        in_specs=[hbm, hbm, hbm, smem, smem],
-        out_specs=(hbm, hbm, hbm),
-        scratch_shapes=[
-            pltpu.VMEM((2, block, hidden), BF16),
-            pltpu.VMEM((2, block, hidden), BF16),
-            pltpu.VMEM((E, block, hidden), BF16),
-            pltpu.VMEM((cap, 2, m, rb, rank), BF16),
-            pltpu.VMEM((E, 2, m, rb, rank), BF16),
-            pltpu.VMEM((E, m, rb, rank), BF16),
-            pltpu.VMEM((E, m, rb, rank), BF16),
-            pltpu.VMEM((E, m - 1, rb, rank), BF16),
-            pltpu.VMEM((E, 2, m, nz, rb, rank), BF16),
-            pltpu.VMEM((E, block, rank), F32),
-            pltpu.VMEM((E, block, rank), BF16),
-            pltpu.VMEM((E, 1, rank), F32),
-            pltpu.VMEM((E, groups - 1, 1, rank), F32),
-            pltpu.VMEM((E, 1, rank), F32),
-            pltpu.VMEM((E, nz - 1, 1, rank), F32),
-            pltpu.VMEM((E, 2, hb, half, LANES), BF16),
-            pltpu.VMEM((E, hb, half, LANES), BF16),
-            pltpu.VMEM((E, 2, a, b, L2, half, LANES), BF16),
-            pltpu.VMEM((E, a - 1, b, L2, half, LANES), BF16),
-            pltpu.VMEM((E, b - 1, a, L2, half, LANES), BF16),
-            pltpu.VMEM((E, b, L2, half, LANES), BF16),
-            pltpu.VMEM((E, a, L2, half, LANES), BF16),
-            pltpu.VMEM((E, b - 1, L2, half, LANES), BF16),
-            pltpu.VMEM((E, a - 1, L2, half, LANES), BF16),
-            pltpu.VMEM((E, L, half, LANES), BF16),
-            pltpu.VMEM((E, nz - 1, nr, LANES), BF16),
-            pltpu.VMEM((E, 2, hb, half, LANES), BF16),
+        in_specs=[hbm] * 5,
+        out_specs=(pl.BlockSpec(memory_space=pltpu.VMEM),) * 3,
+        scratch_shapes=scratch + [
             pltpu.SemaphoreType.DMA((E, total)),
             pltpu.SemaphoreType.DMA((E, total)),
             pltpu.SemaphoreType.DMA((2, 2)),
-            pltpu.SemaphoreType.DMA,
-            pltpu.SemaphoreType.DMA((E,)),
-            pltpu.SemaphoreType.DMA((E,)),
-            pltpu.SemaphoreType.DMA((E,)),
+            pltpu.SMEM((E,), jnp.int32),
+            pltpu.SMEM((groups,), jnp.int32),
+            pltpu.SemaphoreType.DMA((3,)),
         ],
         compiler_params=pltpu.CompilerParams(
-            collective_id=0, has_side_effects=True, vmem_limit_bytes=63_000_000
+            collective_id=0, has_side_effects=True, vmem_limit_bytes=limit
         ),
     )(momentum, gradient, q_view, owner_group, group_counts)
 
@@ -411,12 +462,25 @@
     hb, half = right.shape[2:4]
     own_blocks = share // LANES
 
-    def kernel(owner_ref, counts_ref, comb, left_ref, right_ref, mom_out, upd_out, q_out, kept):
+    def kernel(
+        owner_in, counts_in, comb, left_ref, right_ref, mom_out, upd_out, q_out,
+        kept, owner_ref, counts_ref, small_sem,
+    ):
         e = pl.program_id(0)
+        small = (
+            pltpu.make_async_copy(owner_in, owner_ref, small_sem.at[0]),
+            pltpu.make_async_copy(counts_in, counts_ref, small_sem.at[1]),
+        )
+
+        @pl.when(e == 0)
+        def _():
+            for one in small:
+                one.start()
+
         me, s = lax.axis_index("group"), lax.axis_index("shard")
 
         def block_of(i):
-            return jnp.concatenate([right_ref[0, 0, i], right_ref[0, 1, i]], axis=0).astype(F32)
+            return jnp.concatenate([right_ref[e, 0, i], right_ref[e, 1, i]], axis=0).astype(F32)
 
         squares = jnp.zeros((rank, LANES), F32)
         for i in range(hb):
@@ -424,13 +488,13 @@
             squares = squares + one * one
         scale = lax.rsqrt(jnp.sum(squares, axis=1, keepdims=True) / hidden + stability_offset)
 
-        unit = left_ref[0]
+        unit = left_ref[e]
         for j in range(hb // 2):
             raw = jnp.concatenate([block_of(2 * j), block_of(2 * j + 1)], axis=1)
             span = slice(2 * j * LANES, (2 * j + 2) * LANES)
             low = jnp.dot(unit, raw.astype(BF16), preferred_element_type=F32)
             mom_out[0, :, span] = (
-                comb[0, :, span].astype(F32) - (1.0 - momentum_decay) * low
+                comb[e, :, span].astype(F32) - (1.0 - momentum_decay) * low
             ).astype(BF16)
             new = (raw * scale).astype(BF16)
             upd_out[0, :, span] = (
@@ -440,6 +504,8 @@
         @pl.when(e == 0)
         def _():
             kept[...] = jnp.zeros_like(kept)
+            for one in small:
+                one.wait()
 
         own, slot, at = scalar_slot(owner_ref, e, experts, cap)
 
@@ -454,7 +520,8 @@
                 for i in range(own_blocks):
                     q_out[0, j, i * LANES:(i + 1) * LANES, :] = kept[j, i].T.astype(BF16)
 
-    smem = pl.BlockSpec(memory_space=pltpu.SMEM)
+    hbm = pl.BlockSpec(memory_space=pltpu.HBM)
+    vmem = pl.BlockSpec(memory_space=pltpu.VMEM)
     row = pl.BlockSpec((1, block, hidden), lambda e: (e, 0, 0))
     return pl.pallas_call(
         kernel,
@@ -466,13 +533,18 @@
             jax.ShapeDtypeStruct((1, cap, share, rank), BF16),
         ),
         in_specs=[
-            smem, smem, row,
-            pl.BlockSpec((1, block, rank), lambda e: (e, 0, 0)),
-            pl.BlockSpec((1, 2, hb, half, LANES), lambda e: (e, 0, 0, 0, 0)),
+            hbm, hbm, vmem, vmem, vmem,
         ],
         out_specs=(row, row, pl.BlockSpec((1, cap, share, rank), lambda e: (0, 0, 0, 0))),
-        scratch_shapes=[pltpu.VMEM((cap, own_blocks, rank, LANES), F32)],
-        compiler_params=pltpu.CompilerParams(dimension_semantics=("arbitrary",)),
+        scratch_shapes=[
+            pltpu.VMEM((cap, own_blocks, rank, LANES), F32),
+            pltpu.SMEM(owner_group.shape, jnp.int32),
+            pltpu.SMEM(group_counts.shape, jnp.int32),
+            pltpu.SemaphoreType.DMA((2,)),
+        ],
+        compiler_params=pltpu.CompilerParams(
+            dimension_semantics=("arbitrary",), vmem_limit_bytes=24_000_000
+        ),
     )(owner_group, group_counts, combined, left, right)
 
 

time: 106 us -> 92.8 us (0.88)
  Pallas kernels: 105 us -> 89.6 us
  local copies, waits for them, and re-layouts: 0 us -> 2.3 us
    pallas_call x1, Pallas kernels: 90.3 us -> 79.9 us  [exchange(): pl.pallas_call(kernel, name='exchange', out_shape=(jax.ShapeDtypeStruct((...]
    pallas_call x1, Pallas kernels: 14.6 us -> 9.67 us  [finish(): pl.pallas_call(kernel, name='finish', grid=(experts,), out_shape=(jax.Sha...]
    unnamed x0 -> x6, local copies, waits for them, and re-layouts: none -> 2.3 us
where the time goes in v2:
time: 92.8 us; the launch traced here: 92.6 us
  Pallas kernels  89.6 us (97%)
  local copies, waits for them, and re-layouts  2.3 us (2%)
    pallas_call x1, Pallas kernels, exchange(): pl.pallas_call(kernel, name='exchange', out_shape=(jax.ShapeDtypeStruct((...  79.9 us
    pallas_call x1, Pallas kernels, finish(): pl.pallas_call(kernel, name='finish', grid=(experts,), out_shape=(jax.Sha...  9.67 us
    unnamed x6, local copies, waits for them, and re-layouts  2.3 us

profile of v2, /device:TPU:0, one launch (start us, length us, event | category | flops | bytes accessed | tf_op | source)
XLA Modules:
  0.0 92.6 jit_solution(12739161182897423481)
XLA Ops:
  0.6 0.0 copy-start
  0.6 1.0 %copy-done = bf16[1,3,512,128]{3,2,1,0:T(8,128)(2,1)S(1)} copy-done((bf16[1,3,512,128]{3,2,1,0:T(8,128)(2,1)S(1)}, bf16[1,3,512,128]{3,2,1,0:T(8,128)(2,1)}, u32[]{:S(2)}) %copy-start) | copy-done | bytes 393240
  1.6 0.0 copy-start.1
  1.6 0.7 copy-done.1
  2.3 0.0 copy-start.2
  2.3 0.7 copy-done.2
  2.9 79.9 %exchange.1 = (bf16[8,224,2048]{2,1,0:T(8,128)(2,1)S(1)}, bf16[8,224,128]{2,1,0:T(8,128)(2,1)S(1)}, bf16[8,2,16,64,128]{4,3,2,1,0:T(8,128)(2,1)S(1)}) custom-call(bf16[8,224,2048]{2,1,0:T(8,128)(2,1)} %mom.1, bf16[8,224,2048]{2,1,0:T(8,128)(2,1)} %grad.1, bf16[3,2,4,64,128]{4,3,2,1,0:T(8,128)(2,1)S(1)} %bitcast.1, s32[8]{0:T(128)S(1)} %copy-done.1, ...), custom_call_target="tpu_custom_call" | custom-call | tf_op jit(solution)/shard_map/exchange/pallas_call | solution.py:435
  82.9 9.7 %finish.1 = (bf16[8,224,2048]{2,1,0:T(8,128)(2,1)}, bf16[8,224,2048]{2,1,0:T(8,128)(2,1)}, bf16[1,3,512,128]{3,2,1,0:T(8,128)(2,1)}) custom-call(s32[8]{0:T(128)S(1)} %copy-done.1, s32[8]{0:T(128)S(1)} %copy-done.2, bf16[8,224,2048]{2,1,0:T(8,128)(2,1)S(1)} %get-tuple-element.6.comb, bf16[8,224,128]{2,1,0:T(8,128)(2,1)S(1)} %get-tuple-element.7.left_ref, ...), custom_call_target="tpu_custom_call" | custom-call | tf_op jit(solution)/shard_map/finish/pallas_call | solution.py:526
Async XLA Ops:
  0.6 1.0 %copy-start = (bf16[1,3,512,128]{3,2,1,0:T(8,128)(2,1)S(1)}, bf16[1,3,512,128]{3,2,1,0:T(8,128)(2,1)}, u32[]{:S(2)}) copy-start(bf16[1,3,512,128]{3,2,1,0:T(8,128)(2,1)} %param.7) | copy-start | bytes 1179652
  1.6 0.7 copy-start.1
  2.3 0.7 copy-start.2

commit v3 on v2

--- a/solution.py
+++ b/solution.py
@@ -33,7 +33,7 @@
     return own, slot, jnp.minimum(slot, cap - 1)
 
 
-def exchange(momentum, gradient, q_prev, owner_group, group_counts):
+def exchange(momentum, gradient, q_prev, plan):
     experts, block, hidden = momentum.shape
     cap, share, rank = q_prev.shape[1:]
     groups, nz = lax.axis_size("group"), lax.axis_size("shard")
@@ -42,15 +42,17 @@
     b = m // a
     rb = share // groups
     hb = hidden // LANES
+    own_blocks = share // LANES
     L = hb // m
     L2 = L // 2
     half = rank // 2
     subs = nz // L
     nr = half // subs
     q_view = q_prev.reshape(cap, 2, m, rb, rank)
+    plan_shape = plan.shape
 
     counts = [
-        ("qcore", 1), ("qplane", m - 1), ("qz", nz - 1), ("qxy", a + b - 2),
+        ("qz", nz - 1), ("qxy", a + b - 2),
         ("qdiag", 2 * (a - 1) * (b - 1)), ("qback", 1),
         ("ncore", 1), ("n1", a + b - 2), ("n2", a + b - 2), ("nz", nz - 1),
         ("rcore", 1), ("p1", a + b - 2), ("p2", a + b - 2), ("rz", nz - 1),
@@ -62,12 +64,12 @@
         total += n
 
     def kernel(
-        mom, grad, q_in, owner_in, counts_in,
-        comb, left, right_out,
-        mom_buf, grad_buf, q_own, qp, qc_land, qc, qp_land, Q,
-        left_raw, n_own, nc_land, n_chip, n1_land, n_a, n_b, n2_land, n_place, nz_land, weights,
+        mom, grad, q_ref, plan_in,
+        comb, upd, q_out,
+        mom_buf, grad_buf, slots, Q,
+        left_raw, left, kept, n_own, nc_land, n_chip, n1_land, n_a, n_b, n2_land, n_place, nz_land, weights,
         pt, c_land, cs, p1a, p1b, s2a, s2b, p2a, p2b, ps, z_land, R,
-        send, recv, load_sem, owner_ref, counts_ref, small_sem,
+        send, recv, slot_send, slot_recv, load_sem, plan, plan_sem,
     ):
         g, s = lax.axis_index("group"), lax.axis_index("shard")
         c = lax.rem(g, 2)
@@ -95,13 +97,7 @@
 
         def family(name, e):
             out = []
-            if name == "qcore":
-                out.append((qp.at[e, oc], qc_land.at[e], qc_land.at[e], core))
-            elif name == "qplane":
-                for k in range(1, m):
-                    to = up(p, k, m)
-                    out.append((qc.at[e, to], qp_land.at[e, k - 1], qp_land.at[e, k - 1], (to * 2 + c, s)))
-            elif name == "qz":
+            if name == "qz":
                 for k in range(1, nz):
                     here = Q.at[e, c, p, s]
                     out.append((here, here, Q.at[e, c, p, down(s, k, nz)], (g, up(s, k, nz))))
@@ -198,13 +194,8 @@
                 pltpu.make_async_copy(grad.at[e], grad_buf.at[at], load_sem.at[at, 1]),
             )
 
-        small = [
-            pltpu.make_async_copy(q_in, q_own, small_sem.at[0]),
-            pltpu.make_async_copy(owner_in, owner_ref, small_sem.at[1]),
-            pltpu.make_async_copy(counts_in, counts_ref, small_sem.at[2]),
-        ]
-        for one in small:
-            one.start()
+        plan_load = pltpu.make_async_copy(plan_in, plan, plan_sem)
+        plan_load.start()
         for e in range(min(2, experts)):
             for one in loads(e):
                 one.start()
@@ -215,34 +206,28 @@
         for k in range(1, nz):
             pl.semaphore_signal(barrier, inc=1, device_id=(g, up(s, k, nz)), device_id_type=pl.DeviceIdType.MESH)
 
-        for one in small:
-            one.wait()
+        def slot_copy(k):
+            to = up(g, k, groups)
+            return pltpu.make_async_remote_copy(
+                src_ref=q_ref.at[:, lax.rem(to, 2), to // 2], dst_ref=slots.at[g],
+                send_sem=slot_send.at[k - 1], recv_sem=slot_recv.at[k - 1],
+                device_id=(to, s), device_id_type=pl.DeviceIdType.MESH,
+            )
+
+        slots[g] = q_ref[:, c, p]
+        kept[...] = jnp.zeros_like(kept)
+        plan_load.wait()
+        pl.semaphore_wait(barrier, groups + nz - 2)
+        for k in range(1, groups):
+            slot_copy(k).start()
+        for k in range(1, groups):
+            slot_copy(k).wait_recv()
 
         @pl.loop(0, experts)
         def _(e):
-            own, slot, at = scalar_slot(owner_ref, e, experts, cap)
-            live = (slot < counts_ref[own]) & (own == g)
-            factor = jnp.where(live, 1.0, 0.0).astype(F32)
-            for h in range(2):
-                qp[e, h] = (q_own[at, h].astype(F32) * factor).astype(BF16)
-
-        pl.semaphore_wait(barrier, groups + nz - 2)
-
-        @pl.loop(0, experts)
-        def _(e):
-            start("qcore", e)
-
-        def stage_q0(e):
-            arrived("qcore", e)
-            qc[e] = qp[e, c] + qc_land[e]
-            start("qplane", e)
-
-        def stage_q1(e):
-            arrived("qplane", e)
-            mine = qc[e, p]
-            for k in range(m - 1):
-                mine = mine + qp_land[e, k]
-            Q[e, c, p, s] = mine
+            own, slot, at = scalar_slot(plan, e, experts, cap)
+            factor = jnp.where(slot < plan[experts + own], 1.0, 0.0).astype(F32)
+            Q[e, c, p, s] = (slots[own, at].astype(F32) * factor).astype(BF16)
             start("qz", e)
 
         def stage_combine(e):
@@ -365,47 +350,77 @@
 
         def stage_done(e):
             arrived("gback", e)
-            for h in range(2):
-                right_out[e, h] = R[e, h]
+
+            def block_of(i):
+                return jnp.concatenate([R[e, 0, i], R[e, 1, i]], axis=0).astype(F32)
+
+            squares = jnp.zeros((rank, LANES), F32)
+            for i in range(hb):
+                one = block_of(i)
+                squares = squares + one * one
+            scale = lax.rsqrt(jnp.sum(squares, axis=1, keepdims=True) / hidden + stability_offset)
+
+            unit = left[e]
+            for j in range(hb // 2):
+                raw = jnp.concatenate([block_of(2 * j), block_of(2 * j + 1)], axis=1)
+                span = slice(2 * j * LANES, (2 * j + 2) * LANES)
+                low = jnp.dot(unit, raw.astype(BF16), preferred_element_type=F32)
+                comb[e, :, span] = (
+                    comb[e, :, span].astype(F32) - (1.0 - momentum_decay) * low
+                ).astype(BF16)
+                new = (raw * scale).astype(BF16)
+                upd[e, :, span] = (
+                    jnp.dot(unit, new, preferred_element_type=F32) * math.sqrt(D / RANK)
+                ).astype(BF16)
+
+            own, slot, _ = scalar_slot(plan, e, experts, cap)
+            mine = (slot < plan[experts + own]) & (own == g)
+            for i in range(own_blocks):
+                new = (block_of(s * own_blocks + i) * scale).astype(BF16).astype(F32)
+                for j in range(cap):
+                    kept[j, i] += new * jnp.where(mine & (slot == j), 1.0, 0.0).astype(F32)
+
             for name, _ in counts:
                 sent(name, e)
 
         stages = [
-            (0, stage_q0),
-            (2, stage_q1),
-            (4, relay("qz", "qxy")),
-            (6, relay("qxy", "qdiag")),
-            (8, relay("qdiag", "qback")),
+            (0, relay("qz", "qxy")),
+            (2, relay("qxy", "qdiag")),
+            (4, relay("qdiag", "qback")),
             (0, stage_combine),
-            (9, stage_left),
-            (10, stage_chip),
-            (11, stage_p1),
-            (12, stage_p2),
-            (14, stage_rz),
-            (16, relay("gz", "gxy")),
-            (17, relay("gxy", "gdiag")),
+            (5, stage_left),
+            (6, stage_chip),
+            (8, stage_p1),
+            (10, stage_p2),
+            (12, stage_rz),
+            (14, relay("gz", "gxy")),
+            (16, relay("gxy", "gdiag")),
             (18, relay("gdiag", "gback")),
             (19, stage_done),
         ]
 
-        @pl.loop(0, experts + 19)
+        @pl.loop(0, experts + stages[-1][0])
         def _(t):
             for offset, stage in stages:
                 @pl.when((t >= offset) & (t < offset + experts))
                 def _():
                     stage(t - offset)
 
+        for j in range(cap):
+            for i in range(own_blocks):
+                q_out[0, j, i * LANES:(i + 1) * LANES, :] = kept[j, i].T.astype(BF16)
+        for k in range(1, groups):
+            slot_copy(k).wait_send()
+
     E = experts
     scratch = [
         pltpu.VMEM((2, block, hidden), BF16),
         pltpu.VMEM((2, block, hidden), BF16),
-        pltpu.VMEM((cap, 2, m, rb, rank), BF16),
-        pltpu.VMEM((E, 2, m, rb, rank), BF16),
-        pltpu.VMEM((E, m, rb, rank), BF16),
-        pltpu.VMEM((E, m, rb, rank), BF16),
-        pltpu.VMEM((E, m - 1, rb, rank), BF16),
+        pltpu.VMEM((groups, cap, rb, rank), BF16),
         pltpu.VMEM((E, 2, m, nz, rb, rank), BF16),
         pltpu.VMEM((E, block, rank), F32),
+        pltpu.VMEM((E, block, rank), BF16),
+        pltpu.VMEM((cap, own_blocks, rank, LANES), F32),
         pltpu.VMEM((E, 1, rank), F32),
         pltpu.VMEM((E, 1, rank), F32),
         pltpu.VMEM((E, 1, rank), F32),
@@ -429,129 +444,64 @@
         pltpu.VMEM((E, nz - 1, nr, LANES), BF16),
         pltpu.VMEM((E, 2, hb, half, LANES), BF16),
     ]
-    outputs = 2 * E * (block * (hidden + rank) + hidden * rank)
-    limit = min(VMEM_BYTES, sum(map(vmem_bytes, scratch)) + outputs + 1_500_000)
+    outputs = 2 * (2 * E * block * hidden + cap * share * rank)
+    limit = min(VMEM_BYTES - outputs, sum(map(vmem_bytes, scratch)) + 11_000_000)
     hbm = pl.BlockSpec(memory_space=pltpu.HBM)
     return pl.pallas_call(
         kernel,
         name="exchange",
         out_shape=(
             jax.ShapeDtypeStruct((E, block, hidden), BF16),
-            jax.ShapeDtypeStruct((E, block, rank), BF16),
-            jax.ShapeDtypeStruct((E, 2, hb, half, LANES), BF16),
+            jax.ShapeDtypeStruct((E, block, hidden), BF16),
+            jax.ShapeDtypeStruct((1, cap, share, rank), BF16),
         ),
-        in_specs=[hbm] * 5,
+        in_specs=[hbm, hbm, pl.BlockSpec(memory_space=pltpu.VMEM), hbm],
         out_specs=(pl.BlockSpec(memory_space=pltpu.VMEM),) * 3,
         scratch_shapes=scratch + [
             pltpu.SemaphoreType.DMA((E, total)),
             pltpu.SemaphoreType.DMA((E, total)),
+            pltpu.SemaphoreType.DMA((groups - 1,)),
+            pltpu.SemaphoreType.DMA((groups - 1,)),
             pltpu.SemaphoreType.DMA((2, 2)),
-            pltpu.SMEM((E,), jnp.int32),
-            pltpu.SMEM((groups,), jnp.int32),
-            pltpu.SemaphoreType.DMA((3,)),
+            pltpu.SMEM(plan_shape, jnp.int32),
+            pltpu.SemaphoreType.DMA,
         ],
         compiler_params=pltpu.CompilerParams(
             collective_id=0, has_side_effects=True, vmem_limit_bytes=limit
         ),
-    )(momentum, gradient, q_view, owner_group, group_counts)
-
-
-def finish(combined, left, right, owner_group, group_counts, cap, share):
-    experts, block, hidden = combined.shape
-    rank = left.shape[2]
-    hb, half = right.shape[2:4]
-    own_blocks = share // LANES
-
-    def kernel(
-        owner_in, counts_in, comb, left_ref, right_ref, mom_out, upd_out, q_out,
-        kept, owner_ref, counts_ref, small_sem,
-    ):
-        e = pl.program_id(0)
-        small = (
-            pltpu.make_async_copy(owner_in, owner_ref, small_sem.at[0]),
-            pltpu.make_async_copy(counts_in, counts_ref, small_sem.at[1]),
-        )
-
-        @pl.when(e == 0)
-        def _():
-            for one in small:
-                one.start()
-
-        me, s = lax.axis_index("group"), lax.axis_index("shard")
-
-        def block_of(i):
-            return jnp.concatenate([right_ref[e, 0, i], right_ref[e, 1, i]], axis=0).astype(F32)
-
-        squares = jnp.zeros((rank, LANES), F32)
-        for i in range(hb):
-            one = block_of(i)
-            squares = squares + one * one
-        scale = lax.rsqrt(jnp.sum(squares, axis=1, keepdims=True) / hidden + stability_offset)
-
-        unit = left_ref[e]
-        for j in range(hb // 2):
-            raw = jnp.concatenate([block_of(2 * j), block_of(2 * j + 1)], axis=1)
-            span = slice(2 * j * LANES, (2 * j + 2) * LANES)
-            low = jnp.dot(unit, raw.astype(BF16), preferred_element_type=F32)
-            mom_out[0, :, span] = (
-                comb[e, :, span].astype(F32) - (1.0 - momentum_decay) * low
-            ).astype(BF16)
-            new = (raw * scale).astype(BF16)
-            upd_out[0, :, span] = (
-                jnp.dot(unit, new, preferred_element_type=F32) * math.sqrt(D / RANK)
-            ).astype(BF16)
-
-        @pl.when(e == 0)
-        def _():
-            kept[...] = jnp.zeros_like(kept)
-            for one in small:
-                one.wait()
-
-        own, slot, at = scalar_slot(owner_ref, e, experts, cap)
-
-        @pl.when((slot < counts_ref[own]) & (own == me))
-        def _():
-            for i in range(own_blocks):
-                kept[at, i] = (block_of(s * own_blocks + i) * scale).astype(BF16).astype(F32)
-
-        @pl.when(e == experts - 1)
-        def _():
-            for j in range(cap):
-                for i in range(own_blocks):
-                    q_out[0, j, i * LANES:(i + 1) * LANES, :] = kept[j, i].T.astype(BF16)
-
-    hbm = pl.BlockSpec(memory_space=pltpu.HBM)
-    vmem = pl.BlockSpec(memory_space=pltpu.VMEM)
-    row = pl.BlockSpec((1, block, hidden), lambda e: (e, 0, 0))
+    )(momentum, gradient, q_view, plan)
+
+
+def store(*results):
+    pieces = [one.shape[0] for one in results]
+
+    def kernel(*refs):
+        n = len(results)
+        copies = []
+        for at, count in enumerate(pieces):
+            for e in range(count):
+                copies.append((refs[at].at[e], refs[n + at].at[e]))
+        sems = refs[2 * n]
+        copies = [pltpu.make_async_copy(a, b, sems.at[k]) for k, (a, b) in enumerate(copies)]
+        for one in copies:
+            one.start()
+        for one in copies:
+            one.wait()
+
     return pl.pallas_call(
         kernel,
-        name="finish",
-        grid=(experts,),
-        out_shape=(
-            jax.ShapeDtypeStruct(combined.shape, BF16),
-            jax.ShapeDtypeStruct(combined.shape, BF16),
-            jax.ShapeDtypeStruct((1, cap, share, rank), BF16),
-        ),
-        in_specs=[
-            hbm, hbm, vmem, vmem, vmem,
-        ],
-        out_specs=(row, row, pl.BlockSpec((1, cap, share, rank), lambda e: (0, 0, 0, 0))),
-        scratch_shapes=[
-            pltpu.VMEM((cap, own_blocks, rank, LANES), F32),
-            pltpu.SMEM(owner_group.shape, jnp.int32),
-            pltpu.SMEM(group_counts.shape, jnp.int32),
-            pltpu.SemaphoreType.DMA((2,)),
-        ],
-        compiler_params=pltpu.CompilerParams(
-            dimension_semantics=("arbitrary",), vmem_limit_bytes=24_000_000
-        ),
-    )(owner_group, group_counts, combined, left, right)
+        name="store",
+        out_shape=tuple(jax.ShapeDtypeStruct(one.shape, one.dtype) for one in results),
+        in_specs=[pl.BlockSpec(memory_space=pltpu.VMEM)] * len(results),
+        out_specs=(pl.BlockSpec(memory_space=pltpu.HBM),) * len(results),
+        scratch_shapes=[pltpu.SemaphoreType.DMA((sum(pieces),))],
+        compiler_params=pltpu.CompilerParams(vmem_limit_bytes=24_000_000),
+    )(*results)
 
 
 def shards(momentum, gradient, q_prev, owner_group, group_counts):
-    cap, share = q_prev.shape[1:3]
-    combined, left, right = exchange(momentum, gradient, q_prev, owner_group, group_counts)
-    return finish(combined, left, right, owner_group, group_counts, cap, share)
+    plan = jnp.concatenate([owner_group, group_counts])
+    return store(*exchange(momentum, gradient, q_prev, plan))
 
 
 def solution(mesh):

time: 92.8 us -> 88.8 us (0.957)
  Pallas kernels: 89.6 us -> 86.2 us
  local copies, waits for them, and re-layouts: 2.3 us -> 1 us
    pallas_call x1, Pallas kernels: 9.67 us -> 5.44 us  [store(): pl.pallas_call(kernel, name='store', out_shape=tuple((jax.ShapeDtypeStruc...]
    unnamed x6 -> x2, local copies, waits for them, and re-layouts: 2.3 us -> 1 us
where the time goes in v3:
time: 88.8 us; the launch traced here: 88.6 us
  Pallas kernels  86.2 us (97%)
  local copies, waits for them, and re-layouts  1 us (1%)
    pallas_call x1, Pallas kernels, exchange(): pl.pallas_call(kernel, name='exchange', out_shape=(jax.ShapeDtypeStruct((...  80.8 us
    pallas_call x1, Pallas kernels, store(): pl.pallas_call(kernel, name='store', out_shape=tuple((jax.ShapeDtypeStruc...  5.44 us

profile of v3, /device:TPU:0, one launch (start us, length us, event | category | flops | bytes accessed | tf_op | source)
XLA Modules:
  0.0 88.6 jit_solution(1828204894540069181)
XLA Ops:
  0.6 0.7 pad_add_fusion.plan_in
  1.4 0.0 copy-start
  1.4 1.0 %copy-done = bf16[1,3,512,128]{3,2,1,0:T(8,128)(2,1)S(1)} copy-done((bf16[1,3,512,128]{3,2,1,0:T(8,128)(2,1)S(1)}, bf16[1,3,512,128]{3,2,1,0:T(8,128)(2,1)}, u32[]{:S(2)}) %copy-start) | copy-done | bytes 393240
  2.4 80.8 %exchange.1 = (bf16[8,224,2048]{2,1,0:T(8,128)(2,1)S(1)}, bf16[8,224,2048]{2,1,0:T(8,128)(2,1)S(1)}, bf16[1,3,512,128]{3,2,1,0:T(8,128)(2,1)S(1)}) custom-call(bf16[8,224,2048]{2,1,0:T(8,128)(2,1)} %mom.1, bf16[8,224,2048]{2,1,0:T(8,128)(2,1)} %grad.1, bf16[3,2,4,64,128]{4,3,2,1,0:T(8,128)(2,1)S(1)} %bitcast.1, s32[16]{0:T(128)S(1)} %pad_add_fusion.plan_in), custom_call_target="tpu_custom_call" | custom-call | tf_op jit(solution)/shard_map/exchange/pallas_call | solution.py:450
  83.2 5.4 %store.1 = (bf16[8,224,2048]{2,1,0:T(8,128)(2,1)}, bf16[8,224,2048]{2,1,0:T(8,128)(2,1)}, bf16[1,3,512,128]{3,2,1,0:T(8,128)(2,1)}) custom-call(bf16[8,224,2048]{2,1,0:T(8,128)(2,1)S(1)} %get-tuple-element.6.refs_0_, bf16[8,224,2048]{2,1,0:T(8,128)(2,1)S(1)} %get-tuple-element.7.refs_1_, bf16[1,3,512,128]{3,2,1,0:T(8,128)(2,1)S(1)} %get-tuple-element.8.refs_2_), custom_call_target="tpu_custom_call" | custom-call | tf_op jit(solution)/shard_map/store/pallas_call | solution.py:491
Async XLA Ops:
  1.4 1.0 %copy-start = (bf16[1,3,512,128]{3,2,1,0:T(8,128)(2,1)S(1)}, bf16[1,3,512,128]{3,2,1,0:T(8,128)(2,1)}, u32[]{:S(2)}) copy-start(bf16[1,3,512,128]{3,2,1,0:T(8,128)(2,1)} %param.7) | copy-start | bytes 1179652

commit v4 on v3

--- a/solution.py
+++ b/solution.py
@@ -48,10 +48,12 @@
     half = rank // 2
     subs = nz // L
     nr = half // subs
+    plain = experts - 3 * experts // 8
     q_view = q_prev.reshape(cap, 2, m, rb, rank)
     plan_shape = plan.shape
 
     counts = [
+        ("fxy", a + b - 2), ("fdiag", 2 * (a - 1) * (b - 1)), ("fz", nz - 1),
         ("qz", nz - 1), ("qxy", a + b - 2),
         ("qdiag", 2 * (a - 1) * (b - 1)), ("qback", 1),
         ("ncore", 1), ("n1", a + b - 2), ("n2", a + b - 2), ("nz", nz - 1),
@@ -97,7 +99,17 @@
 
         def family(name, e):
             out = []
-            if name == "qz":
+            if name == "fxy":
+                here = f_place(e, y, x)
+                for k in range(1, a):
+                    out.append((here, here, f_place(e, down(y, k, a), x), dev(up(y, k, a), x)))
+                for k in range(1, b):
+                    out.append((here, here, f_place(e, y, down(x, k, b)), dev(y, up(x, k, b))))
+            elif name == "fz":
+                for k in range(1, nz):
+                    here = Q.at[e, c, :, s]
+                    out.append((here, here, Q.at[e, c, :, down(s, k, nz)], (g, up(s, k, nz))))
+            elif name == "qz":
                 for k in range(1, nz):
                     here = Q.at[e, c, p, s]
                     out.append((here, here, Q.at[e, c, p, down(s, k, nz)], (g, up(s, k, nz))))
@@ -113,8 +125,8 @@
                     out.append((whole(e, y, x), whole(e, y, x), whole(e, down(y, k, a), x), dev(up(y, k, a), x)))
                 for k in range(1, b):
                     out.append((whole(e, y, x), whole(e, y, x), whole(e, y, down(x, k, b)), dev(y, up(x, k, b))))
-            elif name in ("qdiag", "gdiag"):
-                part = q_half if name == "qdiag" else r_half
+            elif name in ("qdiag", "gdiag", "fdiag"):
+                part = {"qdiag": q_half, "gdiag": r_half, "fdiag": f_half}[name]
                 for k in range(1, a):
                     for j in range(1, b):
                         xx = down(x, j, b)
@@ -169,6 +181,12 @@
         def q_half(e, yy, xx, h):
             return Q.at[e, c, yy * b + xx, pl.ds(h * (nz // 2), nz // 2)]
 
+        def f_place(e, yy, xx):
+            return Q.at[e, c, yy * b + xx, s]
+
+        def f_half(e, yy, xx, h):
+            return Q.at[e, c, yy * b + xx, s, pl.ds(h * (rb // 2), rb // 2)]
+
         def r_place(e, yy, xx):
             return R.at[e, c, pl.ds((yy * b + xx) * L, L)]
 
@@ -228,7 +246,14 @@
             own, slot, at = scalar_slot(plan, e, experts, cap)
             factor = jnp.where(slot < plan[experts + own], 1.0, 0.0).astype(F32)
             Q[e, c, p, s] = (slots[own, at].astype(F32) * factor).astype(BF16)
-            start("qz", e)
+
+            @pl.when(e < plain)
+            def _():
+                start("qz", e)
+
+            @pl.when(e >= plain)
+            def _():
+                start("fxy", e)
 
         def stage_combine(e):
             for one in loads(e):
@@ -240,6 +265,30 @@
             def _():
                 for one in loads(e + 2):
                     one.start()
+
+        def plane_first(before, after):
+            @pl.loop(plain, experts)
+            def _(e):
+                arrived(before, e)
+                start(after, e)
+
+        def if_plain(stage):
+            def only(e):
+                @pl.when(e < plain)
+                def _():
+                    stage(e)
+            return only
+
+        def stage_back(e):
+            @pl.when(e < plain)
+            def _():
+                arrived("qdiag", e)
+
+            @pl.when(e >= plain)
+            def _():
+                arrived("fz", e)
+
+            start("qback", e)
 
         def relay(before, after):
             def stage(e):
@@ -380,13 +429,25 @@
                 for j in range(cap):
                     kept[j, i] += new * jnp.where(mine & (slot == j), 1.0, 0.0).astype(F32)
 
+            special = ("qz", "qxy", "qdiag")
             for name, _ in counts:
-                sent(name, e)
+                if name[0] != "f" and name not in special:
+                    sent(name, e)
+
+            @pl.when(e < plain)
+            def _():
+                for name in special:
+                    sent(name, e)
+
+            @pl.when(e >= plain)
+            def _():
+                for name in ("fxy", "fdiag", "fz"):
+                    sent(name, e)
 
         stages = [
-            (0, relay("qz", "qxy")),
-            (2, relay("qxy", "qdiag")),
-            (4, relay("qdiag", "qback")),
+            (0, if_plain(relay("qz", "qxy"))),
+            (2, if_plain(relay("qxy", "qdiag"))),
+            (4, stage_back),
             (0, stage_combine),
             (5, stage_left),
             (6, stage_chip),
@@ -401,6 +462,14 @@
 
         @pl.loop(0, experts + stages[-1][0])
         def _(t):
+            @pl.when(t == 0)
+            def _():
+                plane_first("fxy", "fdiag")
+
+            @pl.when(t == 1)
+            def _():
+                plane_first("fdiag", "fz")
+
             for offset, stage in stages:
                 @pl.when((t >= offset) & (t < offset + experts))
                 def _():

time: 88.8 us -> 87.2 us (0.982)
  Pallas kernels: 86.2 us -> 84.6 us
    pallas_call x1, Pallas kernels: 80.8 us -> 79.2 us  [exchange(): pl.pallas_call(kernel, name='exchange', out_shape=(jax.ShapeDtypeStruct((...]
where the time goes in v4:
time: 87.2 us; the launch traced here: 87 us
  Pallas kernels  84.6 us (97%)
  local copies, waits for them, and re-layouts  1 us (1%)
    pallas_call x1, Pallas kernels, exchange(): pl.pallas_call(kernel, name='exchange', out_shape=(jax.ShapeDtypeStruct((...  79.2 us
    pallas_call x1, Pallas kernels, store(): pl.pallas_call(kernel, name='store', out_shape=tuple((jax.ShapeDtypeStruc...  5.44 us

profile of v4, /device:TPU:0, one launch (start us, length us, event | category | flops | bytes accessed | tf_op | source)
XLA Modules:
  0.0 87.0 jit_solution(7267168978336113208)
XLA Ops:
  0.6 0.7 pad_add_fusion.plan_in
  1.4 0.0 copy-start
  1.4 1.0 %copy-done = bf16[1,3,512,128]{3,2,1,0:T(8,128)(2,1)S(1)} copy-done((bf16[1,3,512,128]{3,2,1,0:T(8,128)(2,1)S(1)}, bf16[1,3,512,128]{3,2,1,0:T(8,128)(2,1)}, u32[]{:S(2)}) %copy-start) | copy-done | bytes 393240
  2.4 79.2 %exchange.1 = (bf16[8,224,2048]{2,1,0:T(8,128)(2,1)S(1)}, bf16[8,224,2048]{2,1,0:T(8,128)(2,1)S(1)}, bf16[1,3,512,128]{3,2,1,0:T(8,128)(2,1)S(1)}) custom-call(bf16[8,224,2048]{2,1,0:T(8,128)(2,1)} %mom.1, bf16[8,224,2048]{2,1,0:T(8,128)(2,1)} %grad.1, bf16[3,2,4,64,128]{4,3,2,1,0:T(8,128)(2,1)S(1)} %bitcast.1, s32[16]{0:T(128)S(1)} %pad_add_fusion.plan_in), custom_call_target="tpu_custom_call" | custom-call | tf_op jit(solution)/shard_map/exchange/pallas_call | solution.py:519
  81.6 5.4 %store.1 = (bf16[8,224,2048]{2,1,0:T(8,128)(2,1)}, bf16[8,224,2048]{2,1,0:T(8,128)(2,1)}, bf16[1,3,512,128]{3,2,1,0:T(8,128)(2,1)}) custom-call(bf16[8,224,2048]{2,1,0:T(8,128)(2,1)S(1)} %get-tuple-element.6.refs_0_, bf16[8,224,2048]{2,1,0:T(8,128)(2,1)S(1)} %get-tuple-element.7.refs_1_, bf16[1,3,512,128]{3,2,1,0:T(8,128)(2,1)S(1)} %get-tuple-element.8.refs_2_), custom_call_target="tpu_custom_call" | custom-call | tf_op jit(solution)/shard_map/store/pallas_call | solution.py:560
Async XLA Ops:
  1.4 1.0 %copy-start = (bf16[1,3,512,128]{3,2,1,0:T(8,128)(2,1)S(1)}, bf16[1,3,512,128]{3,2,1,0:T(8,128)(2,1)}, u32[]{:S(2)}) copy-start(bf16[1,3,512,128]{3,2,1,0:T(8,128)(2,1)} %param.7) | copy-start | bytes 1179652
